TPU v7x, 256 devices: a whole 4x4x8 slice. The times are simulated.
256 devices in a mesh: band: 64 (over x, z_lo, y, core), pw: 4 (over z_hi).
Axes of the slice: x: 4, y: 4, z: 8 (z_hi: 4, z_lo: 2; z = z_hi * 2 + z_lo), core: 2. Of those that a mesh axis runs over, the one named last changes fastest.
Arguments:
- pair_density: bfloat16 [320, 128, 9216], P('band', None, 'pw'), may hold values from -6 to 6
- eigvecs: bfloat16 [2944, 9216], P('band', 'pw'), may hold values from -0.0625 to 0.0625
- screening: bfloat16 [2944, 2944], P('pw'), may hold values from -0.00048828125 to 0.00048828125
- occupation: float32 [128], replicated, may hold values from 0 to 1
- window_start: int32 [320], P('band'), may hold values from 0 to 511, as said below
- window_len: int32 [320], P('band'), may hold values from 1 to 128, as said below
- slot_band: int32 [320], P('band'), may hold values from -1 to 127, as said below
Outputs:
- sigma: float32 [512, 512], P(('band', 'pw'))
Inputs may be any that keep to these rules, and one draw needn't show every extreme that they name: window_start + window_len <= 512 for every slot. `window_len`: some slot has a window of 128 bands. On each index of band the live slots (slot_band >= 0) come first among its 5 slots; each index holds 3 to 5 live slots, and the counts of index i and index i + 64 / 2 add up to 8.
All inputs are finite; a program needn't handle non-finite values.
Results may differ from a plain program's by a relative error of at most 0.0049.
Values may be sent and summed in bfloat16 or wider, within the bound.
A program may use at most 128 MiB of HBM per device.

v0:
```python
import jax
import jax.numpy as jnp
from jax import lax
from jax.sharding import PartitionSpec as P

NB_SIGMA = 512


def from_partner(array, axis, distance):
    return lax.ppermute(array, axis, [(i, i ^ 1 << distance) for i in range(lax.axis_size(axis))])


def in_blocks(array, dim, length):
    lengths = array.shape
    blocks = array.reshape(*lengths[:dim], length, lengths[dim] // length, *lengths[dim + 1 :])
    return jnp.moveaxis(blocks, dim, 0)


def summed_on_arrival(array, axis, dim):
    blocks = in_blocks(array, dim, lax.axis_size(axis))
    arrived = lax.all_to_all(blocks, axis, split_axis=0, concat_axis=0, tiled=True)
    return arrived.astype(jnp.float32).sum(axis=0)


def sum_at_owner(array, axis, dim):
    length = lax.axis_size(axis)
    blocks = lax.all_to_all(in_blocks(array, dim, length), axis, 0, 0, tiled=True)
    return jnp.sum(blocks, axis=0)


def per_device(pair_density, eigvecs, screening, occupation, window_start, window_len, slot_band):
    capacity, block, plane_rows = pair_density.shape
    top_bit = lax.axis_size("band").bit_length() - 2
    live_count = jnp.sum((slot_band >= 0).astype(jnp.int32))
    last = capacity - 1
    spare_meta = jnp.stack([window_start[last], window_len[last], slot_band[last]])
    got_block = from_partner(pair_density[last], "band", top_bit)
    got_meta = from_partner(spare_meta, "band", top_bit)
    taking = live_count == capacity - 2
    kept_density = pair_density[:last]
    density = jnp.where(taking, kept_density.at[last - 1].set(got_block), kept_density)
    starts = jnp.where(
        taking, window_start[:last].at[last - 1].set(got_meta[0]), window_start[:last]
    )
    lengths = jnp.where(taking, window_len[:last].at[last - 1].set(got_meta[1]), window_len[:last])
    band_ids = jnp.where(taking, slot_band[:last].at[last - 1].set(got_meta[2]), slot_band[:last])
    slots = density.shape[0]
    flat = density.reshape(slots * block, plane_rows)
    partial_proj = lax.dot_general(
        flat,
        lax.all_gather(eigvecs, "band", axis=0, tiled=True),
        (((1,), (1,)), ((), ())),
        preferred_element_type=jnp.float32,
    )
    row_ids = jnp.arange(block, dtype=jnp.int32)
    keep_rows = ((row_ids[None, :] < lengths[:, None]) & (band_ids[:, None] >= 0)).astype(
        jnp.float32
    )
    masked = partial_proj * keep_rows.reshape(slots * block, 1)
    share = lax.psum_scatter(masked, "pw", scatter_dimension=1, tiled=True)
    projected = lax.all_gather(share.astype(jnp.bfloat16), "pw", axis=1, tiled=True)
    width = screening.shape[0]
    own_cols = lax.dynamic_slice_in_dim(projected, lax.axis_index("pw") * width, width, 1)
    screened = lax.dot_general(
        projected, screening, (((1,), (1,)), ((), ())), preferred_element_type=jnp.float32
    ).astype(jnp.bfloat16)
    block_sigma = lax.dot_general(
        screened.reshape(slots, block, width),
        own_cols.reshape(slots, block, width),
        (((2,), (2,)), ((0,), (0,))),
        preferred_element_type=jnp.float32,
    )
    band_list = jnp.arange(occupation.shape[0], dtype=jnp.int32)
    weights = 0.5 - jnp.sum(
        jnp.where(band_list[None, :] == band_ids[:, None], occupation[None, :], 0.0), axis=1
    )
    totals = jnp.zeros((NB_SIGMA + block, NB_SIGMA + block), jnp.float32)
    for index in range(slots):
        first = starts[index]
        previous = lax.dynamic_slice(totals, (first, first), (block, block))
        totals = lax.dynamic_update_slice(
            totals, previous + weights[index] * block_sigma[index], (first, first)
        )
    sigma_part = totals[:NB_SIGMA, :NB_SIGMA]
    by_band = summed_on_arrival(sigma_part.astype(jnp.bfloat16), "band", 0)
    return sum_at_owner(by_band, "pw", 0)


def solution(mesh):
    return jax.shard_map(
        per_device,
        mesh=mesh,
        in_specs=(
            P("band", None, "pw"),
            P("band", "pw"),
            P("pw", None),
            P(),
            P("band"),
            P("band"),
            P("band"),
        ),
        out_specs=P(("band", "pw"), None),
        check_vma=False,
    )
```

profile of v0, /device:TPU:1, one launch (start us, length us, event | category | flops | bytes accessed | tf_op | source)
XLA Modules:
  0.0 408.9 jit_solution(6931820106926020516)
XLA Ops:
  7.3 1.3 slice.139
  8.6 1.5 fusion.16
  10.1 2.0 pad_add_fusion
  12.1 3.6 collective-permute-start
  15.7 1.1 slice_bitcast_fusion
  17.1 1.2 slice_bitcast_fusion.1
  18.3 1.3 fusion.14
  22.2 1.2 select_n.61
  24.2 12.2 %collective-permute-done.1 = bf16[128,2304]{1,0:T(8,128)(2,1)S(1)} collective-permute-done((bf16[128,2304]{1,0:T(8,128)(2,1)S(1)}, bf16[128,2304]{1,0:T(8,128)(2,1)S(1)}, u32[]{:S(2)}, u32[]{:S(2)}) %collective-permute-start.1) | collective-permute-done | bytes 589856 | tf_op jit(solution)/shard_map/ppermute | solution.py:10
  36.3 1.2 fusion.4
  37.5 103.1 %all-gather.6.cloned.1.call-done = bf16[64,46,2304]{2,1,0:T(8,128)(2,1)} async-done(((bf16[1,46,2304]{2,1,0:T(8,128)(2,1)}), bf16[64,46,2304]{2,1,0:T(8,128)(2,1)}) %all-gather.6.cloned.1.call-update) | async-done | bytes 13565968 | tf_op jit(solution)/shard_map/all_gather | solution.py:51
  140.7 16.9 %reshape.157 = bf16[2944,2304]{1,0:T(8,128)(2,1)} reshape(bf16[64,46,2304]{2,1,0:T(8,128)(2,1)} %all-gather.6.cloned.1.call-done) | data formatting | bytes 27131904
  157.6 12.1 %convolution_multiply_fusion = f32[512,2944]{0,1:T(8,128)} fusion(bf16[512,2304]{1,0:T(8,128)(2,1)S(1)} %bitcast.53, bf16[2944,2304]{1,0:T(8,128)(2,1)} %reshape.157, f32[512]{0:T(512)S(1)} %convert_bitcast_fusion), kind=kOutput, calls=%fused_computation | convolution fusion | flops 6947274752 | bytes 21956608 | tf_op jit(solution)/shard_map/dot_general | solution.py:49
  169.8 115.1 %reduce-scatter.2.cloned.1.call-done = f32[512,736]{0,1:T(8,128)} async-done(((f32[512,2944]{0,1:T(8,128)}), f32[512,736]{0,1:T(8,128)}) %reduce-scatter.2.cloned.1.call-update) | async-done | bytes 1507344 | tf_op jit(solution)/shard_map/reduce_scatter | solution.py:60
  284.9 2.4 convert_element_type.26
  295.0 51.6 %all-gather.4.cloned.1.call-done = bf16[512,2944]{0,1:T(8,128)(2,1)} async-done(((bf16[512,736]{0,1:T(8,128)(2,1)}), bf16[512,2944]{0,1:T(8,128)(2,1)}) %all-gather.4.cloned.1.call-update) | async-done | bytes 3014672 | tf_op jit(solution)/shard_map/all_gather | solution.py:61
  346.6 1.2 constant_dynamic-slice_fusion
  348.1 5.7 %fusion = bf16[92,4,8,128]{3,2,1,0:T(8,128)(2,1)S(1)} fusion(bf16[736,2944]{1,0:T(8,128)(2,1)} %param.17, bf16[512,2944]{0,1:T(8,128)(2,1)} %all-gather.4.cloned.1.call-done), kind=kOutput, calls=%fused_computation.2 | convolution fusion | flops 2219163648 | bytes 8101888 | tf_op jit(solution)/shard_map/dot_general | solution.py:64
  354.8 1.8 dynamic_update_slice.12
  357.3 2.1 dynamic_update_slice.13
  360.1 2.1 dynamic_update_slice.14
  362.9 2.1 dynamic_update_slice.15
  365.1 26.8 %all_to_all.10 = bf16[64,8,512]{2,1,0:T(8,128)(2,1)S(1)} all-to-all(bf16[64,8,512]{2,1,0:T(8,128)(2,1)S(1)} %fusion.5), channel_id=1, replica_groups=mesh['band'=64,'pw'=4] {'band'}, dimensions={0} | all-to-all | bytes 1048576 | tf_op jit(solution)/shard_map/all_to_all | solution.py:21
  392.0 9.7 %all_to_all.11 = f32[4,2,512]{2,1,0:T(2,128)S(1)} all-to-all(f32[4,2,512]{2,1,0:T(2,128)S(1)} %reshape.154), channel_id=1, replica_groups=mesh['band'=64,'pw'=4] {'pw'}, dimensions={0} | all-to-all | bytes 32768 | tf_op jit(solution)/shard_map/all_to_all | solution.py:27
  (34 shorter events, 7.6 us)
Async XLA Ops:
  6.5 134.1 %all-gather.6.cloned.1.call-start = ((), (), s32[]{:S(2)}) async-start(), calls=%async_computation.5 | async-start | bytes 14376960 | tf_op jit(solution)/shard_map/all_gather | solution.py:51
  7.3 277.6 %reduce-scatter.2.cloned.1.call-start = ((), (), s32[]{:S(2)}) async-start(), calls=%async_computation.3 | async-start | bytes 7536640 | tf_op jit(solution)/shard_map/reduce_scatter | solution.py:60
  12.1 7.5 %copy-start = (s32[5]{0:T(128)S(1)}, s32[5]{0:T(128)}, u32[]{:S(2)}) copy-start(s32[5]{0:T(128)} %param.20) | copy-start | bytes 64
  12.1 24.2 %slice-start = ((bf16[5,128,2304]{2,1,0:T(8,128)(2,1)}), bf16[4,128,2304]{2,1,0:T(8,128)(2,1)S(1)}, s32[]{:S(2)}) async-start(bf16[5,128,2304]{2,1,0:T(8,128)(2,1)} %param.15), calls=%async_computation.6 | async-start | bytes 4718592 | tf_op jit(solution)/shard_map/slice | solution.py:40
  12.1 8.1 %collective-permute-start = (s32[3]{0:T(128)S(1)}, s32[3]{0:T(128)S(1)}, u32[]{:S(2)}, u32[]{:S(2)}) collective-permute-start(s32[3]{0:T(128)S(1)} %pad_add_fusion), channel_id=1, source_target_pairs={{0,128},{4,132},{8,136},{12,140},{16,144},{20,148},{24,152},{28,15... | collective-permute-start | bytes 44 | tf_op jit(solution)/shard_map/ppermute | solution.py:10
  16.9 19.5 %collective-permute-start.1 = (bf16[128,2304]{1,0:T(8,128)(2,1)S(1)}, bf16[128,2304]{1,0:T(8,128)(2,1)S(1)}, u32[]{:S(2)}, u32[]{:S(2)}) collective-permute-start(bf16[128,2304]{1,0:T(8,128)(2,1)S(1)} %slice_bitcast_fusion), channel_id=1, source_target_pairs={{0,128},{4,132},{8,136},{12,140},{16,144},{20,148},{24,152},{28,15... | collective-permute-start | bytes 1769480 | tf_op jit(solution)/shard_map/ppermute | solution.py:10
  169.7 124.5 %copy-start.1 = (f32[128]{0:T(128)S(1)}, f32[128]{0:T(128)}, u32[]{:S(2)}) copy-start(f32[128]{0:T(128)} %param.18) | copy-start | bytes 1540
  169.7 124.5 %copy-start.2 = (s32[4,1]{0,1:T(1,128)S(1)}, s32[4,1]{0,1:T(1,128)}, u32[]{:S(2)}) copy-start(s32[4,1]{0,1:T(1,128)} %select_n.61) | copy-start | bytes 52
  169.7 176.9 %all-gather.4.cloned.1.call-start = ((), (), s32[]{:S(2)}) async-start(), calls=%async_computation.4 | async-start | bytes 3768320 | tf_op jit(solution)/shard_map/all_gather | solution.py:61
Sparse Core Ops, SparseCore 0:
  9.2 131.4 all-gather.5
  169.8 115.0 reduce-scatter.1
  287.4 59.1 all-gather.3
where the time goes:
time: 410 us; the launch traced here: 409 us
  waiting for transfers between devices  283 us (69%)
  blocking collectives  36.6 us (9%)
  local copies, waits for them, and re-layouts  33.5 us (8%)
  between operations  22.1 us (5%)
  matrix products  18.1 us (4%)
  other arithmetic  11.9 us (3%)
    reduce_scatter x1, waiting for transfers between devices, per_device(): share = lax.psum_scatter(masked, 'pw', scatter_dimension=1, tiled=True)  115 us
    all_gather x1, waiting for transfers between devices, per_device(): lax.all_gather(eigvecs, 'band', axis=0, tiled=True)  103 us
    all_gather x1, waiting for transfers between devices, per_device(): lax.all_gather(share.astype(jnp.bfloat16), 'pw', axis=1, tiled=True)  51.6 us
    all_to_all x1, blocking collectives, summed_on_arrival(): lax.all_to_all(blocks, axis, split_axis=0, concat_axis=0, tiled=True)  26.8 us
    unnamed x8, local copies, waits for them, and re-layouts  17 us
    ppermute x2, waiting for transfers between devices, from_partner(): lax.ppermute(array, axis, [(i, i ^ 1 << distance) for i in range(lax.axis...  12.2 us
    dot_general x1, matrix products, per_device(): lax.dot_general(flat, lax.all_gather(eigvecs, 'band', axis=0, tiled=True)...  12.1 us
    all_to_all x1, blocking collectives, sum_at_owner(): lax.all_to_all(in_blocks(array, dim, length), axis, 0, 0, tiled=True)  9.74 us
  transfers between devices with their start and end apart: 5, of which 4 were waited for; matrix products, arithmetic and copies ran while one was open for 3% of the time, Pallas kernels for 0%

commit v1 on v0

v1 whole, which is shorter than its diff:
```python
import jax
import jax.numpy as jnp
from jax import lax
from jax.experimental import pallas as pl
from jax.experimental.pallas import tpu as pltpu
from jax.sharding import PartitionSpec as P

NB_SIGMA = 512
BLOCK = 128
F32 = jnp.float32
BF16 = jnp.bfloat16
SHARE, PADDED = 46, 48
CHUNK = 8 * PADDED
WROWS, WCOLS = 96, 768

N_COPIES = 160


def main_kernel(
    taking_ref,
    meta_ref,
    a_ref,
    eig_ref,
    w_ref,
    bs_ref,
    meta_out,
    a_all,
    spare,
    own3,
    bbuf,
    wbuf,
    part,
    hop_s,
    hop_r,
    dir_s,
    dir_r,
    comb_s,
    comb_r,
    pt,
    ptd,
    pth,
    scr,
    meta_buf,
    ssem,
    rsem,
    lsem,
):
    band = lax.axis_index("band")
    h = lax.axis_index("pw")
    x = band // 16
    zl = (band // 8) % 2
    y = (band // 2) % 4
    c = band % 2
    u = x * (1 - c) + y * c
    v = y * (1 - c) + x * c
    su = 16 - 14 * c
    sv = 2 + 14 * c
    hp, hm, h2 = (h + 1) % 4, (h + 3) % 4, (h + 2) % 4
    up, um, u2 = (u + 1) % 4, (u + 3) % 4, (u + 2) % 4
    vp, vm, v2 = (v + 1) % 4, (v + 3) % 4, (v + 2) % 4

    def at_uv(uu, vv):
        return (uu * su + vv * sv + zl * 8 + c, h)

    dev_up, dev_um = at_uv(up, v), at_uv(um, v)
    dev_vp, dev_vm = at_uv(u, vp), at_uv(u, vm)
    dev_hp, dev_hm = (band, hp), (band, hm)
    dev_zl = (x * 16 + (1 - zl) * 8 + y * 2 + c, h)
    dev_mate = (x * 16 + zl * 8 + y * 2 + 1 - c, h)
    dev_far = (((x + 2) % 4) * 16 + zl * 8 + y * 2 + c, h)

    barrier = pltpu.get_barrier_semaphore()
    peers = [dev_up, dev_um, dev_vp, dev_vm, dev_hp, dev_hm, dev_zl, dev_mate, dev_far]
    for peer in peers:
        pl.semaphore_signal(barrier, inc=1, device_id=peer, device_id_type=pl.DeviceIdType.MESH)
    pl.semaphore_wait(barrier, len(peers))

    ids = {}
    sent = []

    def remote(name, src, dst, device):
        i = ids.setdefault(name, len(ids))
        return pltpu.make_async_remote_copy(
            src_ref=src,
            dst_ref=dst,
            send_sem=ssem.at[i],
            recv_sem=rsem.at[i],
            device_id=device,
            device_id_type=pl.DeviceIdType.MESH,
        )

    def send(name, src, dst, device):
        copy = remote(name, src, dst, device)
        copy.start()
        sent.append(copy)

    def got(name, landing, device):
        remote(name, landing, landing, device).wait_recv()

    local_ids = {}

    def local(name, src, dst):
        i = local_ids.setdefault(name, len(local_ids))
        return pltpu.make_async_copy(src, dst, lsem.at[i])

    send("zl", eig_ref, bbuf.at[v, u, zl], dev_zl)
    own_b = local("b", eig_ref, bbuf.at[v, u, zl])
    own_b.start()
    send("spare", a_ref.at[4], spare, dev_far)
    send("meta_far", meta_ref, meta_buf.at[1], dev_far)
    send("meta_mate", meta_ref, meta_buf.at[2], dev_mate)
    own_a = []
    for j in range(3):
        own_a.append(local(f"a{j}", a_ref.at[j], a_all.at[2 * j + c]))
        own_a[-1].start()
        send(f"mate_a{j}", a_ref.at[j], a_all.at[2 * j + c], dev_mate)
    own_a.append(local("a3", a_ref.at[3], own3))
    own_a[-1].start()

    def w_slice(p, q):
        row = pl.multiple_of(c * 368 + p * WROWS - 16 * (p // 3), 16)
        col = pl.multiple_of(q * WCOLS - 128 * (q // 3), 128)
        return w_ref.at[pl.ds(row, WROWS), pl.ds(col, WCOLS)]

    send("wz_m", w_slice(u, v), wbuf.at[1, u, v], dev_hm)
    send("wz_p", w_slice(u, v), wbuf.at[3, u, v], dev_hp)
    own_w = []
    for p in range(4):
        for q in range(4):
            own_w.append(local(f"w{p}{q}", w_slice(p, q), wbuf.at[0, p, q]))
            own_w[-1].start()

    own_b.wait()
    got("zl", bbuf.at[v, u, 1 - zl], dev_zl)

    def v_send(kind, buf_at, uu, tag):
        send(f"{kind}v_p{tag}", buf_at(uu, v), buf_at(uu, v), dev_vp)
        send(f"{kind}v_m{tag}", buf_at(uu, v), buf_at(uu, v), dev_vm)

    def b_at(uu, vv):
        return bbuf.at[vv, uu]

    def w_at(uu, vv):
        return wbuf.at[pl.ds(1, 3), uu, vv]

    send("bu_p", b_at(u, v), b_at(u, v), dev_up)
    send("bu_m", b_at(u, v), b_at(u, v), dev_um)
    v_send("b", b_at, u, 0)
    got("bu_p", b_at(um, v), dev_um)
    send("buf_p", bbuf.at[v, um, 0], bbuf.at[v, um, 0], dev_up)
    v_send("b", b_at, um, 1)
    got("bu_m", b_at(up, v), dev_up)
    send("buf_m", bbuf.at[v, up, 1], bbuf.at[v, up, 1], dev_um)
    v_send("b", b_at, up, 2)

    lower, upper = pl.ds(0, WROWS // 2), pl.ds(WROWS // 2, WROWS // 2)
    got("wz_m", wbuf.at[1, u, v], dev_hp)
    send("wzf_m", wbuf.at[1, u, v, lower], wbuf.at[2, u, v, lower], dev_hm)
    got("wz_p", wbuf.at[3, u, v], dev_hm)
    send("wzf_p", wbuf.at[3, u, v, upper], wbuf.at[2, u, v, upper], dev_hp)

    got("buf_p", bbuf.at[v, u2, 0], dev_um)
    got("buf_m", bbuf.at[v, u2, 1], dev_up)
    v_send("b", b_at, u2, 3)

    got("meta_far", meta_buf.at[1], dev_far)
    send("meta_mate_far", meta_buf.at[1], meta_buf.at[3], dev_mate)
    got("spare", spare, dev_far)
    own_a[3].wait()
    taking = taking_ref[0] == 1
    a_all[6 + c] = jnp.where(taking, spare[...], own3[...])
    send("mate_a3", a_all.at[6 + c], a_all.at[6 + c], dev_mate)

    got("wzf_m", wbuf.at[2, u, v, lower], dev_hp)
    got("wzf_p", wbuf.at[2, u, v, upper], dev_hm)
    send("wu_p", w_at(u, v), w_at(u, v), dev_up)
    send("wu_m", w_at(u, v), w_at(u, v), dev_um)

    for j in range(3):
        own_a[j].wait()
        got(f"mate_a{j}", a_all.at[2 * j + 1 - c], dev_mate)
    got("mate_a3", a_all.at[7 - c], dev_mate)

    left, right = pl.ds(0, BLOCK), pl.ds(BLOCK, BLOCK)

    def compute(k, vk):
        @pl.loop(0, 4)
        def _(d):
            part[k, d] = lax.dot_general(
                bbuf[vk].reshape(CHUNK, bbuf.shape[-1]),
                a_all[pl.ds(2 * d, 2)].reshape(2 * BLOCK, bbuf.shape[-1]),
                (((1,), (1,)), ((), ())),
                preferred_element_type=F32,
            )

        hop_s[k, 0] = part[k, h2, :, left].astype(BF16)
        send(f"hop{k}0", hop_s.at[k, 0], hop_r.at[k, 0], dev_hm)
        hop_s[k, 1] = part[k, h2, :, right].astype(BF16)
        send(f"hop{k}1", hop_s.at[k, 1], hop_r.at[k, 1], dev_hp)
        dir_s[k, 0] = part[k, hm, :, right].astype(BF16)
        send(f"dir{k}0", dir_s.at[k, 0], dir_r.at[k, 0], dev_hm)
        dir_s[k, 1] = part[k, hp, :, left].astype(BF16)
        send(f"dir{k}1", dir_s.at[k, 1], dir_r.at[k, 1], dev_hp)

    def combine(k):
        got(f"hop{k}0", hop_r.at[k, 0], dev_hp)
        comb_s[k, 0] = (part[k, hm, :, left] + hop_r[k, 0].astype(F32)).astype(BF16)
        send(f"comb{k}0", comb_s.at[k, 0], comb_r.at[k, 0], dev_hm)
        got(f"hop{k}1", hop_r.at[k, 1], dev_hm)
        comb_s[k, 1] = (part[k, hp, :, right] + hop_r[k, 1].astype(F32)).astype(BF16)
        send(f"comb{k}1", comb_s.at[k, 1], comb_r.at[k, 1], dev_hp)

    def finish(k, vk):
        got(f"dir{k}0", dir_r.at[k, 0], dev_hp)
        got(f"dir{k}1", dir_r.at[k, 1], dev_hm)
        got(f"comb{k}0", comb_r.at[k, 0], dev_hp)
        got(f"comb{k}1", comb_r.at[k, 1], dev_hm)
        pt[c, vk, :, left] = part[k, h, :, left] + (
            comb_r[k, 0].astype(F32) + dir_r[k, 1].astype(F32)
        )
        pt[c, vk, :, right] = part[k, h, :, right] + (
            comb_r[k, 1].astype(F32) + dir_r[k, 0].astype(F32)
        )
        send(f"pt{k}", pt.at[c, vk], pt.at[c, vk], dev_mate)

    compute(0, v)

    around = (u, um, up, u2)
    for tag in range(4):
        got(f"bv_p{tag}", b_at(around[tag], vm), dev_vm)
        if tag < 2:
            send(f"bvf_p{tag}", b_at(around[tag], vm), b_at(around[tag], vm), dev_vp)
    for tag in range(4):
        got(f"bv_m{tag}", b_at(around[tag], vp), dev_vp)
        if tag >= 2:
            send(f"bvf_m{tag}", b_at(around[tag], vp), b_at(around[tag], vp), dev_vm)

    v_send("w", w_at, u, 0)
    three = pl.ds(1, 3)
    got("wu_p", w_at(um, v), dev_um)
    send("wuf_p", wbuf.at[three, um, v, lower], wbuf.at[three, um, v, lower], dev_up)
    v_send("w", w_at, um, 1)
    got("wu_m", w_at(up, v), dev_up)
    send("wuf_m", wbuf.at[three, up, v, upper], wbuf.at[three, up, v, upper], dev_um)
    v_send("w", w_at, up, 2)

    compute(1, vm)
    combine(0)
    compute(2, vp)
    combine(1)
    finish(0, v)

    got("wuf_p", wbuf.at[three, u2, v, lower], dev_um)
    got("wuf_m", wbuf.at[three, u2, v, upper], dev_up)
    v_send("w", w_at, u2, 3)

    for tag in range(4):
        if tag < 2:
            got(f"bvf_p{tag}", b_at(around[tag], v2), dev_vm)
        else:
            got(f"bvf_m{tag}", b_at(around[tag], v2), dev_vp)
    compute(3, v2)
    combine(2)
    finish(1, vm)
    combine(3)

    for tag in range(4):
        got(f"wv_p{tag}", w_at(around[tag], vm), dev_vm)
        if tag < 2:
            send(f"wvf_p{tag}", w_at(around[tag], vm), w_at(around[tag], vm), dev_vp)
    for tag in range(4):
        got(f"wv_m{tag}", w_at(around[tag], vp), dev_vp)
        if tag >= 2:
            send(f"wvf_m{tag}", w_at(around[tag], vp), w_at(around[tag], vp), dev_vm)

    finish(2, vp)
    finish(3, v2)
    order = (v, vm, vp, v2)
    for k in range(4):
        got(f"pt{k}", pt.at[1 - c, order[k]], dev_mate)

    for src in range(2):
        for vv in range(4):
            for uu in range(4):
                for zz in range(2):
                    xx, yy = (uu, vv) if src == 0 else (vv, uu)
                    first = SHARE * (xx * 16 + zz * 8 + yy * 2 + src)
                    row = PADDED * (2 * uu + zz)
                    ptd[first : first + SHARE, :] = pt[src, vv, row : row + SHARE, :]
    pth[...] = ptd[...].astype(BF16)

    for copy in own_w:
        copy.wait()
    for tag in range(4):
        if tag < 2:
            got(f"wvf_p{tag}", w_at(around[tag], v2), dev_vm)
        else:
            got(f"wvf_m{tag}", w_at(around[tag], v2), dev_vp)

    for q in range(4):
        skip = 128 if q == 3 else 0

        @pl.loop(0, 4)
        def _(rel):
            value = jnp.dot(
                wbuf[rel, :, q, :, skip:].reshape(4 * WROWS, WCOLS - skip),
                pth[WCOLS * q : WCOLS * (q + 1) - skip, :],
                preferred_element_type=F32,
            )
            if q == 0:
                scr[rel] = value
            else:
                scr[rel] += value

    for slot in range(2):
        lanes = pl.ds(slot * BLOCK, BLOCK)
        total = jnp.zeros((BLOCK, BLOCK), F32)
        for rel in range(4):
            base = ((h + rel) % 4) * 736 + c * 368
            for skip, first, count in ((0, 0, 288), (304, 288, 80)):
                rows = pl.ds(pl.multiple_of(base + first, 16), count)
                total += lax.dot_general(
                    scr[rel, pl.ds(skip, count), lanes],
                    ptd[rows, lanes],
                    (((0,), (0,)), ((), ())),
                    preferred_element_type=F32,
                    precision=lax.Precision.HIGHEST,
                )
        bs_ref[slot] = total

    got("meta_mate", meta_buf.at[2], dev_mate)
    got("meta_mate_far", meta_buf.at[3], dev_mate)
    meta_out[0] = meta_ref[...]
    for i in range(1, 4):
        meta_out[i] = meta_buf[i]
    for copy in sent:
        copy.wait_send()
    assert len(ids) <= N_COPIES


def summed_on_arrival(array, axis, dim):
    length = lax.axis_size(axis)
    lengths = array.shape
    blocks = array.reshape(*lengths[:dim], length, lengths[dim] // length, *lengths[dim + 1 :])
    blocks = jnp.moveaxis(blocks, dim, 0)
    arrived = lax.all_to_all(blocks, axis, split_axis=0, concat_axis=0, tiled=True)
    return arrived.astype(F32).sum(axis=0)


def per_device(pair_density, eigvecs, screening, occupation, window_start, window_len, slot_band):
    capacity, block, plane_rows = pair_density.shape
    live_count = jnp.sum((slot_band >= 0).astype(jnp.int32))
    taking = (live_count == capacity - 2).astype(jnp.int32).reshape(1)
    meta = jnp.pad(
        jnp.stack([window_start, window_len, slot_band]), ((0, 5), (0, 128 - capacity))
    )
    eig = jnp.pad(eigvecs, ((0, PADDED - SHARE), (0, 0)))
    width = screening.shape[1]
    vmem = pl.BlockSpec(memory_space=pltpu.VMEM)
    hbm = pl.BlockSpec(memory_space=pltpu.HBM)
    scratch = [
        pltpu.VMEM((8, block, plane_rows), BF16),
        pltpu.VMEM((block, plane_rows), BF16),
        pltpu.VMEM((block, plane_rows), BF16),
        pltpu.VMEM((4, 4, 2, PADDED, plane_rows), BF16),
        pltpu.VMEM((4, 4, 4, WROWS, WCOLS), BF16),
        pltpu.VMEM((4, 4, CHUNK, 2 * block), F32),
    ]
    scratch += [pltpu.VMEM((4, 2, CHUNK, block), BF16)] * 6
    scratch += [
        pltpu.VMEM((2, 4, CHUNK, 2 * block), F32),
        pltpu.VMEM((width, 2 * block), F32),
        pltpu.VMEM((width, 2 * block), BF16),
        pltpu.VMEM((4, 4 * WROWS, 2 * block), F32),
        pltpu.VMEM((4, 8, 128), jnp.int32),
        pltpu.SemaphoreType.DMA((N_COPIES,)),
        pltpu.SemaphoreType.DMA((N_COPIES,)),
        pltpu.SemaphoreType.DMA((24,)),
    ]
    block_sigma, metas = pl.pallas_call(
        main_kernel,
        out_shape=(
            jax.ShapeDtypeStruct((2, block, block), F32),
            jax.ShapeDtypeStruct((4, 8, 128), jnp.int32),
        ),
        in_specs=[pl.BlockSpec(memory_space=pltpu.SMEM), vmem, hbm, hbm, hbm],
        out_specs=(vmem, vmem),
        scratch_shapes=scratch,
        compiler_params=pltpu.CompilerParams(
            collective_id=0, has_side_effects=True, vmem_limit_bytes=60 * 1024 * 1024
        ),
        name="project_and_screen",
    )(taking, meta, pair_density, eig, screening)

    core = lax.axis_index("band") % 2
    index = lax.axis_index("pw")
    last = capacity - 1
    totals = jnp.zeros((NB_SIGMA + block, NB_SIGMA + block), F32)
    row_ids = jnp.arange(block, dtype=jnp.int32)
    band_list = jnp.arange(occupation.shape[0], dtype=jnp.int32)
    for slot in range(2):
        is_own = core == slot
        own = jnp.where(is_own, metas[0], metas[2])
        far = jnp.where(is_own, metas[1], metas[3])
        count = jnp.sum((own[2, :capacity] >= 0).astype(jnp.int32))
        swap = (count == capacity - 2) & (index == last - 1)
        mine = lax.dynamic_slice(own, (0, index), (8, 1))[:, 0]
        chosen = jnp.where(swap, far[:, last], mine)
        first, length, band_id = chosen[0], chosen[1], chosen[2]
        keep = ((row_ids < length) & (band_id >= 0)).astype(F32)
        weight = 0.5 - jnp.sum(jnp.where(band_list == band_id, occupation, 0.0))
        piece = block_sigma[slot] * (weight * keep[:, None] * keep[None, :])
        previous = lax.dynamic_slice(totals, (first, first), (block, block))
        totals = lax.dynamic_update_slice(totals, previous + piece, (first, first))
    sigma_part = totals[:NB_SIGMA, :NB_SIGMA]
    by_band = summed_on_arrival(sigma_part.astype(BF16), "band", 0)
    return summed_on_arrival(by_band, "pw", 0)


def solution(mesh):
    return jax.shard_map(
        per_device,
        mesh=mesh,
        in_specs=(
            P("band", None, "pw"),
            P("band", "pw"),
            P("pw", None),
            P(),
            P("band"),
            P("band"),
            P("band"),
        ),
        out_specs=P(("band", "pw"), None),
        check_vma=False,
    )
```

time: 410 us -> 176 us (0.43)
  waiting for transfers between devices: 283 us -> 0 us
  Pallas kernels: 0 us -> 117 us
  local copies, waits for them, and re-layouts: 33.5 us -> 7.33 us
  matrix products: 18.1 us -> 0 us
  between operations: 22.1 us -> 8.57 us
  blocking collectives: 36.6 us -> 32.1 us
    all_gather x2 -> x0, waiting for transfers between devices: 155 us -> none  [the longest x1 103 us: per_device(): lax.all_gather(eigvecs, 'band', axis=0, tiled=True)]
    pallas_call x0 -> x1, Pallas kernels: none -> 117 us  [per_device(): pl.pallas_call(main_kernel, out_shape=(jax.ShapeDtypeStruct((2, block, bl...]
    reduce_scatter x1 -> x0, waiting for transfers between devices: 115 us -> none  [per_device(): share = lax.psum_scatter(masked, 'pw', scatter_dimension=1, tiled=True)]
    dot_general x3 -> x0, matrix products: 18.1 us -> none  [the longest x1 12.1 us: per_device(): lax.dot_general(flat, lax.all_gather(eigvecs, 'band', axis=0, tiled=True)...]
    unnamed x8 -> x4, local copies, waits for them, and re-layouts: 17 us -> 0.01 us
    ppermute x2 -> x0, waiting for transfers between devices: 12.2 us -> none  [from_partner(): lax.ppermute(array, axis, [(i, i ^ 1 << distance) for i in range(lax.axis...]
    all_to_all x1 -> x0, blocking collectives: 9.74 us -> none  [sum_at_owner(): lax.all_to_all(in_blocks(array, dim, length), axis, 0, 0, tiled=True)]
    all_to_all x1 -> x2, blocking collectives: 26.8 us -> 32.1 us  [summed_on_arrival(): lax.all_to_all(blocks, axis, split_axis=0, concat_axis=0, tiled=True)]
  transfers between devices with their start and end apart: 5 -> 0, of which waited for: 4 -> 0; matrix products, arithmetic and copies ran while one was open for 3% -> 0% of each run, Pallas kernels for 0% -> 0%
where the time goes in v1:
time: 176 us; the launch traced here: 175 us
  Pallas kernels  117 us (66%)
  blocking collectives  32.1 us (18%)
  other arithmetic  9.57 us (5%)
  between operations  8.57 us (5%)
  local copies, waits for them, and re-layouts  7.33 us (4%)
    pallas_call x1, Pallas kernels, per_device(): pl.pallas_call(main_kernel, out_shape=(jax.ShapeDtypeStruct((2, block, bl...  117 us
    all_to_all x2, blocking collectives, summed_on_arrival(): lax.all_to_all(blocks, axis, split_axis=0, concat_axis=0, tiled=True)  32.1 us
    dynamic_update_slice x2, local copies, waits for them, and re-layouts, per_device(): totals = lax.dynamic_update_slice(totals, previous + piece, (first, first))  3.76 us

profile of v1, /device:TPU:1, one launch (start us, length us, event | category | flops | bytes accessed | tf_op | source)
XLA Modules:
  0.0 175.1 jit_solution(5639081723873508293)
XLA Ops:
  0.0 1.3 fusion.2
  1.9 0.7 pad_add_fusion
  2.6 0.6 pad.8.meta_ref
  3.2 1.6 pad.9.eig_ref
  4.9 117.5 %project_and_screen.1 = (f32[2,128,128]{2,1,0:T(8,128)}, s32[4,8,128]{2,1,0:T(8,128)}) custom-call(s32[1]{0:T(128)} %bitcast.taking_ref, s32[8,128]{1,0:T(8,128)} %pad.8.meta_ref, bf16[5,128,2304]{2,1,0:T(8,128)(2,1)} %a_ref.1, bf16[48,2304]{1,0:T(8,128)(2,1)} %pad.9.eig_ref, bf16[736,2944]{1,0:T(8,128)(2,1)} %w_ref.1), custom_call_target="tpu_custom_call" | custom-call | tf_op jit(solution)/shard_map/project_and_screen/pallas_call | solution.py:380
  122.4 0.7 select_bitcast_fusion
  123.1 0.7 fusion.3
  125.3 0.6 fusion.9
  127.3 0.1 bitcast_select_fusion.1
  127.3 0.6 fusion.10
  130.4 1.8 %fusion.6 = (f32[]{:T(128)}, f32[]{:T(128)}) fusion(f32[128]{0:T(128)S(1)} %copy-done.1, s32[]{:T(128)} %bitcast.17, s32[]{:T(128)} %bitcast.9), kind=kLoop, calls=%fused_computation.24 | loop fusion | flops 766 | bytes 528 | tf_op jit(solution)/shard_map/reduce_sum | solution.py:411
  133.5 0.6 fusion.8
  134.0 0.6 broadcast_select_fusion
  134.6 0.6 fusion.7
  135.3 0.6 broadcast_select_fusion.1
  137.2 0.9 bitcast_multiply_fusion.1
  138.2 0.1 broadcast_in_dim.12
  138.3 1.7 dynamic_update_slice.6
  140.0 0.1 fusion.1
  140.1 2.1 %dynamic_update_slice.7 = f32[640,640]{1,0:T(8,128)S(1)} dynamic-update-slice(f32[640,640]{1,0:T(8,128)S(1)} %dynamic_update_slice.6, f32[128,128]{1,0:T(8,128)S(1)} %fusion.1, s32[]{:T(128)S(6)} %select_n.96, s32[]{:T(128)S(6)} %select_n.96) | dynamic-update-slice | bytes 131076 | tf_op jit(solution)/shard_map/dynamic_update_slice | solution.py:414
  142.2 21.9 %all_to_all.10 = bf16[64,8,512]{2,1,0:T(8,128)(2,1)S(1)} all-to-all(bf16[64,8,512]{2,1,0:T(8,128)(2,1)S(1)} %fusion), channel_id=1, replica_groups=mesh['band'=64,'pw'=4] {'band'}, dimensions={0} | all-to-all | bytes 1048576 | tf_op jit(solution)/shard_map/all_to_all | solution.py:346
  164.2 0.1 convert_reduce_fusion
  164.3 10.2 %all_to_all.11 = f32[4,2,512]{2,1,0:T(2,128)S(1)} all-to-all(f32[4,2,512]{2,1,0:T(2,128)S(1)} %reshape.72), channel_id=1, replica_groups=mesh['band'=64,'pw'=4] {'pw'}, dimensions={0} | all-to-all | bytes 32768 | tf_op jit(solution)/shard_map/all_to_all | solution.py:346
  174.5 0.6 reduce_sum.69
  (7 shorter events, 0.2 us)
Async XLA Ops:
  4.9 125.6 %copy-start.1 = (f32[128]{0:T(128)S(1)}, f32[128]{0:T(128)}, u32[]{:S(2)}) copy-start(f32[128]{0:T(128)} %param.10) | copy-start | bytes 1540
  122.4 17.6 %copy-start = (f32[2,128,128]{2,1,0:T(8,128)S(1)}, f32[2,128,128]{2,1,0:T(8,128)}, u32[]{:S(2)}) copy-start(f32[2,128,128]{2,1,0:T(8,128)} %get-tuple-element.7) | copy-start | bytes 393220

commit v2 on v1

--- a/solution.py
+++ b/solution.py
@@ -17,13 +17,14 @@
 
 
 def main_kernel(
-    taking_ref,
-    meta_ref,
+    start_ref,
+    len_ref,
+    slot_ref,
+    occ_ref,
     a_ref,
     eig_ref,
     w_ref,
-    bs_ref,
-    meta_out,
+    out_ref,
     a_all,
     spare,
     own3,
@@ -41,6 +42,12 @@
     pth,
     scr,
     meta_buf,
+    bs_own,
+    bs_mate,
+    plane_s,
+    plane_r,
+    line_s,
+    line_r,
     ssem,
     rsem,
     lsem,
@@ -70,7 +77,19 @@
     dev_far = (((x + 2) % 4) * 16 + zl * 8 + y * 2 + c, h)
 
     barrier = pltpu.get_barrier_semaphore()
-    peers = [dev_up, dev_um, dev_vp, dev_vm, dev_hp, dev_hm, dev_zl, dev_mate, dev_far]
+    plane = {}
+    for dx in range(4):
+        for dy in range(4):
+            if dx or dy:
+                place = ((x + dx) % 4, (y + dy) % 4)
+                plane[dx, dy] = place, (place[0] * 16 + zl * 8 + place[1] * 2 + c, h)
+    line = {}
+    for dz in range(2):
+        for dh in range(4):
+            if dz or dh:
+                place = ((zl + dz) % 2, (h + dh) % 4)
+                line[dz, dh] = place, (x * 16 + place[0] * 8 + y * 2 + c, place[1])
+    peers = [dev_mate] + [device for _, device in [*plane.values(), *line.values()]]
     for peer in peers:
         pl.semaphore_signal(barrier, inc=1, device_id=peer, device_id_type=pl.DeviceIdType.MESH)
     pl.semaphore_wait(barrier, len(peers))
@@ -107,8 +126,6 @@
     own_b = local("b", eig_ref, bbuf.at[v, u, zl])
     own_b.start()
     send("spare", a_ref.at[4], spare, dev_far)
-    send("meta_far", meta_ref, meta_buf.at[1], dev_far)
-    send("meta_mate", meta_ref, meta_buf.at[2], dev_mate)
     own_a = []
     for j in range(3):
         own_a.append(local(f"a{j}", a_ref.at[j], a_all.at[2 * j + c]))
@@ -163,11 +180,21 @@
     got("buf_m", bbuf.at[v, u2, 1], dev_up)
     v_send("b", b_at, u2, 3)
 
+    lane = lax.broadcasted_iota(jnp.int32, (1, BLOCK), 1)
+    for j in range(5):
+        kept = (lane < len_ref[j]) & (slot_ref[j] >= 0)
+        meta_buf[0, j : j + 1, :] = jnp.where(kept, start_ref[j] + lane, -1).astype(F32)
+        value = jnp.sum(jnp.where(lane == slot_ref[j], occ_ref[...], 0.0), axis=1, keepdims=True)
+        meta_buf[0, 8 + j : 9 + j, :] = jnp.broadcast_to(0.5 - value, (1, BLOCK))
+    taking = slot_ref[3] < 0
+    meta_buf[0, 5:6, :] = jnp.where(taking, 1.0, 0.0) + jnp.zeros((1, BLOCK), F32)
+
+    send("meta_far", meta_buf.at[0], meta_buf.at[1], dev_far)
+    send("meta_mate", meta_buf.at[0], meta_buf.at[2], dev_mate)
     got("meta_far", meta_buf.at[1], dev_far)
     send("meta_mate_far", meta_buf.at[1], meta_buf.at[3], dev_mate)
     got("spare", spare, dev_far)
     own_a[3].wait()
-    taking = taking_ref[0] == 1
     a_all[6 + c] = jnp.where(taking, spare[...], own3[...])
     send("mate_a3", a_all.at[6 + c], a_all.at[6 + c], dev_mate)
 
@@ -326,34 +353,66 @@
                     preferred_element_type=F32,
                     precision=lax.Precision.HIGHEST,
                 )
-        bs_ref[slot] = total
-
+        bs_own[slot] = total
+
+    send("bs", bs_own, bs_mate, dev_mate)
     got("meta_mate", meta_buf.at[2], dev_mate)
     got("meta_mate_far", meta_buf.at[3], dev_mate)
-    meta_out[0] = meta_ref[...]
-    for i in range(1, 4):
-        meta_out[i] = meta_buf[i]
+    item = lax.broadcasted_iota(jnp.int32, (NB_SIGMA // 2, BLOCK), 0)
+    rows = (item // 64) * 128 + (item // 8) % 2 * 64 + (item // 16) % 4 * 16 + c * 8 + item % 8
+    rows = rows.astype(F32)
+    columns = lax.broadcasted_iota(jnp.int32, (NB_SIGMA, BLOCK), 0).astype(F32)
+    on_last = h == 3
+    places = []
+    for slot in range(2):
+        own = jnp.where(c == slot, 0, 2)
+        swap = (meta_buf[own, 5:6, :] > 0.5) & on_last
+        index = jnp.where(swap, meta_buf[own + 1, 4:5, :], meta_buf[own, pl.ds(h, 1), :])
+        weight = jnp.where(swap, meta_buf[own + 1, 12:13, :], meta_buf[own, pl.ds(8 + h, 1), :])
+        places.append(((rows == index).astype(F32), (columns == index).astype(F32), weight))
+    got("bs", bs_mate, dev_mate)
+    spread = jnp.zeros((NB_SIGMA // 2, NB_SIGMA), F32)
+    for slot in range(2):
+        to_rows, to_columns, weight = places[slot]
+        wide = lax.dot_general(
+            (bs_own[slot] + bs_mate[slot]) * weight,
+            to_columns,
+            (((1,), (1,)), ((), ())),
+            preferred_element_type=F32,
+            precision=lax.Precision.HIGHEST,
+        )
+        spread += jnp.dot(
+            to_rows, wide, preferred_element_type=F32, precision=lax.Precision.HIGHEST
+        )
+    plane_s[...] = spread.astype(BF16).reshape(4, 4, 16, NB_SIGMA)
+    for (dx, dy), (place, device) in plane.items():
+        send(f"plane{dx}{dy}", plane_s.at[place[0], place[1]], plane_r.at[x, y], device)
+    total = plane_s[x, y].astype(F32)
+    for dx, dy in plane:
+        source = (x + 4 - dx) % 4, (y + 4 - dy) % 4
+        landed = plane_r.at[source[0], source[1]]
+        got(f"plane{dx}{dy}", landed, plane[(4 - dx) % 4, (4 - dy) % 4][1])
+        total += landed[...].astype(F32)
+    for zz in range(2):
+        for hh in range(4):
+            first = 8 * zz + 2 * hh
+            line_s[zz, hh] = total[first : first + 2, :]
+    for (dz, dh), (place, device) in line.items():
+        send(f"line{dz}{dh}", line_s.at[place[0], place[1]], line_r.at[zl, h], device)
+    result = line_s[zl, h]
+    for dz, dh in line:
+        source = (zl + dz) % 2, (h + 4 - dh) % 4
+        landed = line_r.at[source[0], source[1]]
+        got(f"line{dz}{dh}", landed, line[dz, (4 - dh) % 4][1])
+        result += landed[...]
+    out_ref[...] = result
     for copy in sent:
         copy.wait_send()
     assert len(ids) <= N_COPIES
 
 
-def summed_on_arrival(array, axis, dim):
-    length = lax.axis_size(axis)
-    lengths = array.shape
-    blocks = array.reshape(*lengths[:dim], length, lengths[dim] // length, *lengths[dim + 1 :])
-    blocks = jnp.moveaxis(blocks, dim, 0)
-    arrived = lax.all_to_all(blocks, axis, split_axis=0, concat_axis=0, tiled=True)
-    return arrived.astype(F32).sum(axis=0)
-
-
 def per_device(pair_density, eigvecs, screening, occupation, window_start, window_len, slot_band):
-    capacity, block, plane_rows = pair_density.shape
-    live_count = jnp.sum((slot_band >= 0).astype(jnp.int32))
-    taking = (live_count == capacity - 2).astype(jnp.int32).reshape(1)
-    meta = jnp.pad(
-        jnp.stack([window_start, window_len, slot_band]), ((0, 5), (0, 128 - capacity))
-    )
+    block, plane_rows = pair_density.shape[1:]
     eig = jnp.pad(eigvecs, ((0, PADDED - SHARE), (0, 0)))
     width = screening.shape[1]
     vmem = pl.BlockSpec(memory_space=pltpu.VMEM)
@@ -372,49 +431,37 @@
         pltpu.VMEM((width, 2 * block), F32),
         pltpu.VMEM((width, 2 * block), BF16),
         pltpu.VMEM((4, 4 * WROWS, 2 * block), F32),
-        pltpu.VMEM((4, 8, 128), jnp.int32),
+        pltpu.VMEM((4, 16, block), F32),
+        pltpu.VMEM((2, block, block), F32),
+        pltpu.VMEM((2, block, block), F32),
+        pltpu.VMEM((4, 4, 16, NB_SIGMA), BF16),
+        pltpu.VMEM((4, 4, 16, NB_SIGMA), BF16),
+        pltpu.VMEM((2, 4, 2, NB_SIGMA), F32),
+        pltpu.VMEM((2, 4, 2, NB_SIGMA), F32),
         pltpu.SemaphoreType.DMA((N_COPIES,)),
         pltpu.SemaphoreType.DMA((N_COPIES,)),
         pltpu.SemaphoreType.DMA((24,)),
     ]
-    block_sigma, metas = pl.pallas_call(
+    smem = pl.BlockSpec(memory_space=pltpu.SMEM)
+    return pl.pallas_call(
         main_kernel,
-        out_shape=(
-            jax.ShapeDtypeStruct((2, block, block), F32),
-            jax.ShapeDtypeStruct((4, 8, 128), jnp.int32),
-        ),
-        in_specs=[pl.BlockSpec(memory_space=pltpu.SMEM), vmem, hbm, hbm, hbm],
-        out_specs=(vmem, vmem),
+        out_shape=jax.ShapeDtypeStruct((2, NB_SIGMA), F32),
+        in_specs=[smem, smem, smem, vmem, hbm, hbm, hbm],
+        out_specs=vmem,
         scratch_shapes=scratch,
         compiler_params=pltpu.CompilerParams(
             collective_id=0, has_side_effects=True, vmem_limit_bytes=60 * 1024 * 1024
         ),
-        name="project_and_screen",
-    )(taking, meta, pair_density, eig, screening)
-
-    core = lax.axis_index("band") % 2
-    index = lax.axis_index("pw")
-    last = capacity - 1
-    totals = jnp.zeros((NB_SIGMA + block, NB_SIGMA + block), F32)
-    row_ids = jnp.arange(block, dtype=jnp.int32)
-    band_list = jnp.arange(occupation.shape[0], dtype=jnp.int32)
-    for slot in range(2):
-        is_own = core == slot
-        own = jnp.where(is_own, metas[0], metas[2])
-        far = jnp.where(is_own, metas[1], metas[3])
-        count = jnp.sum((own[2, :capacity] >= 0).astype(jnp.int32))
-        swap = (count == capacity - 2) & (index == last - 1)
-        mine = lax.dynamic_slice(own, (0, index), (8, 1))[:, 0]
-        chosen = jnp.where(swap, far[:, last], mine)
-        first, length, band_id = chosen[0], chosen[1], chosen[2]
-        keep = ((row_ids < length) & (band_id >= 0)).astype(F32)
-        weight = 0.5 - jnp.sum(jnp.where(band_list == band_id, occupation, 0.0))
-        piece = block_sigma[slot] * (weight * keep[:, None] * keep[None, :])
-        previous = lax.dynamic_slice(totals, (first, first), (block, block))
-        totals = lax.dynamic_update_slice(totals, previous + piece, (first, first))
-    sigma_part = totals[:NB_SIGMA, :NB_SIGMA]
-    by_band = summed_on_arrival(sigma_part.astype(BF16), "band", 0)
-    return summed_on_arrival(by_band, "pw", 0)
+        name="cohsex",
+    )(
+        window_start,
+        window_len,
+        slot_band,
+        occupation.reshape(1, -1),
+        pair_density,
+        eig,
+        screening,
+    )
 
 
 def solution(mesh):

time: 176 us -> 143 us (0.81)
  blocking collectives: 32.1 us -> 0 us
  Pallas kernels: 117 us -> 140 us
  other arithmetic: 9.57 us -> 0 us
  between operations: 8.57 us -> 0.01 us
  local copies, waits for them, and re-layouts: 7.33 us -> 2.89 us
    all_to_all x2 -> x0, blocking collectives: 32.1 us -> none  [summed_on_arrival(): lax.all_to_all(blocks, axis, split_axis=0, concat_axis=0, tiled=True)]
    pallas_call x1, Pallas kernels: 117 us -> 140 us  [per_device(): pl.pallas_call(main_kernel, out_shape=jax.ShapeDtypeStruct((2, NB_SIGMA),...]
    reduce_sum x5 -> x0, other arithmetic: 4.56 us -> none  [the longest x1 1.85 us: per_device(): weight = 0.5 - jnp.sum(jnp.where(band_list == band_id, occupation, 0.0))]
    dynamic_update_slice x2 -> x0, local copies, waits for them, and re-layouts: 3.76 us -> none  [per_device(): totals = lax.dynamic_update_slice(totals, previous + piece, (first, first))]
    mul x3 -> x0, other arithmetic: 2.12 us -> none  [per_device(): piece = block_sigma[slot] * (weight * keep[:, None] * keep[None, :])]
where the time goes in v2:
time: 143 us
  Pallas kernels  140 us (98%)
  local copies, waits for them, and re-layouts  2.89 us (2%)
    pallas_call x1, Pallas kernels, per_device(): pl.pallas_call(main_kernel, out_shape=jax.ShapeDtypeStruct((2, NB_SIGMA),...  140 us

profile of v2, /device:TPU:1, one launch (start us, length us, event | category | flops | bytes accessed | tf_op | source)
XLA Modules:
  0.0 143.3 jit_solution(6870516238178589594)
XLA Ops:
  0.0 1.6 %pad.4.eig_ref = bf16[48,2304]{1,0:T(8,128)(2,1)} pad(bf16[46,2304]{1,0:T(8,128)(2,1)} %param.8, bf16[]{:T(256)} %constant.2.clone.1), padding=0_2x0_0 | pad | bytes 433154 | tf_op jit(solution)/shard_map/jit(_pad)/pad | solution.py:416
  1.6 140.4 %cohsex.1 = f32[2,512]{1,0:T(2,128)} custom-call(s32[5]{0:T(128)} %start_ref.1, s32[5]{0:T(128)} %len_ref.1, s32[5]{0:T(128)} %slot_ref.1, f32[1,128]{1,0:T(1,128)} %bitcast.1, bf16[5,128,2304]{2,1,0:T(8,128)(2,1)} %a_ref.1, bf16[48,2304]{1,0:T(8,128)(2,1)} %pad.4.eig_ref, bf16[736,2944]{1,0:T(8,128)(2,1)} %w_ref.1), custom_call_target="tpu_custom_call" | custom-call | tf_op jit(solution)/shard_map/cohsex/pallas_call | solution.py:446
  142.0 1.3 copy.9

commit v3 on v2

v3 whole, which is shorter than its diff:
```python
import jax
import jax.numpy as jnp
from jax import lax
from jax.experimental import pallas as pl
from jax.experimental.pallas import tpu as pltpu
from jax.sharding import PartitionSpec as P

NB_SIGMA = 512
BLOCK = 128
F32 = jnp.float32
BF16 = jnp.bfloat16
HIGHEST = lax.Precision.HIGHEST
SHARE, PADDED = 46, 48
PIECE = 2 * PADDED
CHUNKS = ((0, 4), (4, 6), (6, 10), (10, 12), (12, 16))


def place_of(kv, ku):
    if kv == 0:
        return ku
    return 12 + ku if kv == 3 else 3 + 2 * ku + kv


WROWS, WCOLS = 96, 768
N_COPIES = 200
scope = jax.named_scope


def main_kernel(
    start_ref,
    len_ref,
    slot_ref,
    occ_ref,
    a_ref,
    eig_ref,
    w_ref,
    out_ref,
    a_all,
    spare,
    relay,
    own3,
    bbuf,
    wbuf,
    part,
    hop_s,
    hop_r,
    dir_s,
    dir_r,
    comb_s,
    comb_r,
    pt,
    ptd,
    pth,
    scr,
    meta_buf,
    meta_all,
    bs_own,
    bs_mate,
    plane_s,
    plane_r,
    line_s,
    line_r,
    ssem,
    rsem,
    lsem,
):
    band = lax.axis_index("band")
    h = lax.axis_index("pw")
    x = band // 16
    zl = (band // 8) % 2
    y = (band // 2) % 4
    c = band % 2
    u = x * (1 - c) + y * c
    v = y * (1 - c) + x * c
    su = 16 - 14 * c
    sv = 2 + 14 * c
    hp, hm, h2 = (h + 1) % 4, (h + 3) % 4, (h + 2) % 4
    up, um, u2 = (u + 1) % 4, (u + 3) % 4, (u + 2) % 4
    vp, vm, v2 = (v + 1) % 4, (v + 3) % 4, (v + 2) % 4

    def at_uv(uu, vv):
        return (uu * su + vv * sv + zl * 8 + c, h)

    dev_up, dev_um = at_uv(up, v), at_uv(um, v)
    dev_vp, dev_vm = at_uv(u, vp), at_uv(u, vm)
    dev_hp, dev_hm = (band, hp), (band, hm)
    dev_zl = (x * 16 + (1 - zl) * 8 + y * 2 + c, h)
    dev_mate = (x * 16 + zl * 8 + y * 2 + 1 - c, h)
    dev_far = (((x + 2) % 4) * 16 + zl * 8 + y * 2 + c, h)

    barrier = pltpu.get_barrier_semaphore()
    plane = {}
    for dx in range(4):
        for dy in range(4):
            if dx or dy:
                place = ((x + dx) % 4, (y + dy) % 4)
                plane[dx, dy] = place, (place[0] * 16 + zl * 8 + place[1] * 2 + c, h)
    line = {}
    for dz in range(2):
        for dh in range(4):
            if dz or dh:
                place = ((zl + dz) % 2, (h + dh) % 4)
                line[dz, dh] = place, (x * 16 + place[0] * 8 + y * 2 + c, place[1])
    dev_xp, dev_xm = plane[1, 0][1], plane[3, 0][1]
    peers = [dev_mate] + [device for _, device in [*plane.values(), *line.values()]]
    for peer in peers:
        pl.semaphore_signal(barrier, inc=1, device_id=peer, device_id_type=pl.DeviceIdType.MESH)

    lane = lax.broadcasted_iota(jnp.int32, (1, BLOCK), 1)
    for j in range(5):
        kept = (lane < len_ref[j]) & (slot_ref[j] >= 0)
        meta_buf[0, j : j + 1, :] = jnp.where(kept, start_ref[j] + lane, -1).astype(F32)
        value = jnp.sum(jnp.where(lane == slot_ref[j], occ_ref[...], 0.0), axis=1, keepdims=True)
        meta_buf[0, 8 + j : 9 + j, :] = jnp.broadcast_to(0.5 - value, (1, BLOCK))
    taking = slot_ref[3] < 0
    meta_buf[0, 5:6, :] = jnp.where(taking, 1.0, 0.0) + jnp.zeros((1, BLOCK), F32)
    with scope('barrier'):
        pl.semaphore_wait(barrier, len(peers))

    ids = {}
    sent = []
    sent_by_core = ([], [])

    def remote(name, src, dst, device):
        i = ids.setdefault(name, len(ids))
        return pltpu.make_async_remote_copy(
            src_ref=src,
            dst_ref=dst,
            send_sem=ssem.at[i],
            recv_sem=rsem.at[i],
            device_id=device,
            device_id_type=pl.DeviceIdType.MESH,
        )

    def send(name, src, dst, device, into=sent):
        copy = remote(name, src, dst, device)
        copy.start()
        into.append(copy if into is sent else (name, device))

    def got(name, landing, device):
        with scope("got_" + name):
            remote(name, landing, landing, device).wait_recv()

    local_ids = {}

    def local(name, src, dst):
        i = local_ids.setdefault(name, len(local_ids))
        copy = pltpu.make_async_copy(src, dst, lsem.at[i])
        copy.start()
        return copy

    oz = 1 - zl
    around = (u, um, up, u2)
    order = (v, vm, vp, v2)

    def b_half(kv, ku, zz):
        return bbuf.at[place_of(kv, ku), zz]

    def b_at(kv, ku):
        return bbuf.at[place_of(kv, ku)]

    three = pl.ds(1, 3)
    lower, upper = pl.ds(0, WCOLS // 2), pl.ds(WCOLS // 2, WCOLS // 2)

    def w_at(uu, vv):
        return wbuf.at[three, uu, vv]

    def w_slice(p, q):
        row = pl.multiple_of(c * 368 + p * WROWS - 16 * (p // 3), 16)
        col = pl.multiple_of(q * WCOLS - 128 * (q // 3), 128)
        return w_ref.at[pl.ds(row, WROWS), pl.ds(col, WCOLS)]

    def w_send(uu, tag):
        send(f"wv_p{tag}", w_at(uu, v), w_at(uu, v), dev_vp)
        send(f"wv_m{tag}", w_at(uu, v), w_at(uu, v), dev_vm)

    def b_send(ku):
        send(f"bv_p{ku}", b_at(0, ku), b_at(1, ku), dev_vp)
        send(f"bv_m{ku}", b_at(0, ku), b_at(2, ku), dev_vm)

    def b_got(kv, ku):
        if ku:
            got(f"bv_{'pm'[kv - 1]}{ku}", b_at(kv, ku), dev_vm if kv == 1 else dev_vp)
        else:
            for zz, tag in ((zl, "a"), (oz, "b")):
                device = dev_vm if kv == 1 else dev_vp
                got(f"bv_{'pm'[kv - 1]}0{tag}", b_half(kv, 0, zz), device)

    def far_line(step):
        def core0():
            for kv, ku in (((1, 0),), ((1, 1), (2, 2)), ((2, 3),), ())[step]:
                device = dev_vp if kv == 1 else dev_vm
                send(f"bf{kv}{ku}", b_at(kv, ku), b_at(3, ku), device, sent_by_core[0])
            if step == 3:
                for ku in range(4):
                    got(f"bf{1 if ku < 2 else 2}{ku}", b_at(3, ku), dev_vm if ku < 2 else dev_vp)

        def core1():
            into = sent_by_core[1]
            if step == 0:
                send("bx_p", b_half(1, 0, zl), b_half(3, 0, zl), dev_vp, into)
                send("bx_m", b_half(2, 0, oz), b_half(3, 0, oz), dev_vm, into)
            elif step == 1:
                got("bx_p", b_half(3, 0, zl), dev_vm)
                got("bx_m", b_half(3, 0, oz), dev_vp)
                send("by_p", b_at(3, 0), b_at(3, 1), dev_up, into)
                send("by_m", b_at(3, 0), b_at(3, 2), dev_um, into)
            elif step == 2:
                got("by_p", b_at(3, 1), dev_um)
                send("byf_p", b_half(3, 1, zl), b_half(3, 3, zl), dev_up, into)
                got("by_m", b_at(3, 2), dev_up)
                send("byf_m", b_half(3, 2, oz), b_half(3, 3, oz), dev_um, into)
            else:
                got("byf_p", b_half(3, 3, zl), dev_um)
                got("byf_m", b_half(3, 3, oz), dev_up)

        pl.when(c == 0)(core0)
        pl.when(c == 1)(core1)

    send("zl", eig_ref, b_half(0, 0, zl), dev_zl)
    own_b = local("b", eig_ref, b_half(0, 0, zl))
    send("bu_p0", eig_ref, b_half(0, 1, zl), dev_up)
    send("bu_m0", eig_ref, b_half(0, 2, zl), dev_um)
    send("meta_far", meta_buf.at[0], meta_buf.at[1], dev_far)
    own_a = []
    for j in range(3):
        own_a.append(local(f"a{j}", a_ref.at[j], a_all.at[2 * j + c]))
        send(f"mate_a{j}", a_ref.at[j], a_all.at[2 * j + c], dev_mate)
    own_a.append(local("a3", a_ref.at[3], own3))
    send("bv_p0a", eig_ref, b_half(1, 0, zl), dev_vp)
    send("bv_m0a", eig_ref, b_half(2, 0, zl), dev_vm)

    got("zl", b_half(0, 0, oz), dev_zl)
    send("bu_p1", b_half(0, 0, oz), b_half(0, 1, oz), dev_up)
    send("bu_m1", b_half(0, 0, oz), b_half(0, 2, oz), dev_um)
    send("bv_p0b", b_half(0, 0, oz), b_half(1, 0, oz), dev_vp)
    send("bv_m0b", b_half(0, 0, oz), b_half(2, 0, oz), dev_vm)
    send("wz_m", w_slice(u, v), wbuf.at[1, u, v], dev_hm)
    send("wz_p", w_slice(u, v), wbuf.at[3, u, v], dev_hp)

    got("bu_p0", b_half(0, 1, zl), dev_um)
    send("buf_p", b_half(0, 1, zl), b_half(0, 3, zl), dev_up)
    got("bu_m0", b_half(0, 2, zl), dev_up)
    got("bu_m1", b_half(0, 2, oz), dev_up)
    send("buf_m", b_half(0, 2, oz), b_half(0, 3, oz), dev_um)
    near, far = pl.ds(0, BLOCK // 2), pl.ds(BLOCK // 2, BLOCK // 2)
    send("spare_p", a_ref.at[4, near], relay.at[0], dev_xp)
    send("spare_m", a_ref.at[4, far], relay.at[1], dev_xm)
    got("bu_p1", b_half(0, 1, oz), dev_um)
    b_send(1)
    b_send(2)
    got("wz_m", wbuf.at[1, u, v], dev_hp)
    send("wzf_m", wbuf.at[1, u, v, :, lower], wbuf.at[2, u, v, :, lower], dev_hm)
    got("wz_p", wbuf.at[3, u, v], dev_hm)
    send("wzf_p", wbuf.at[3, u, v, :, upper], wbuf.at[2, u, v, :, upper], dev_hp)
    own_b.wait()
    for j in range(3):
        own_a[j].wait()
        got(f"mate_a{j}", a_all.at[2 * j + 1 - c], dev_mate)
    got("buf_p", b_half(0, 3, zl), dev_um)
    got("buf_m", b_half(0, 3, oz), dev_up)

    def slot_of(r, cc):
        return (h + r + 7 - 2 * cc - zl) % 4

    def half(cc):
        return pl.ds(cc * BLOCK, BLOCK)

    def project(k, j):
        lo, hi = CHUNKS[k]
        rows = (hi - lo) * PIECE
        part[j, lo:hi] = lax.dot_general(
            bbuf[lo:hi].reshape(rows, bbuf.shape[-1]),
            a_all[pl.ds(2 * j, 2)].reshape(2 * BLOCK, bbuf.shape[-1]),
            (((1,), (1,)), ((), ())),
            preferred_element_type=F32,
        ).reshape(hi - lo, PIECE, 2 * BLOCK)

    def span(k):
        return pl.ds(CHUNKS[k][0], CHUNKS[k][1] - CHUNKS[k][0])

    def phase(late, j, run):
        pl.when((j == 3) if late else (j != 3))(run)

    def compute(k, late):
        with scope(f"compute{k}_{late}"):
            if late:
                project(k, 3)
            else:

                @pl.loop(0, 3)
                def _(j):
                    project(k, j)

            for name, i, r, cc, send_buf, recv_buf, device in (
                ("hop", 0, 2, 0, hop_s, hop_r, dev_hm),
                ("hop", 1, 2, 1, hop_s, hop_r, dev_hp),
                ("dir", 0, 3, 1, dir_s, dir_r, dev_hm),
                ("dir", 1, 1, 0, dir_s, dir_r, dev_hp),
            ):
                j = slot_of(r, cc)
                copy = remote(
                    f"{name}{k}{i}", send_buf.at[i, span(k)], recv_buf.at[i, span(k)], device
                )
                if not late:
                    sent.append(copy)

                def run():
                    send_buf[i, span(k)] = part[j, span(k), :, half(cc)].astype(BF16)
                    copy.start()

                phase(late, j, run)

    def combine(k, late, core=None):
        for i, r, cc, source, device in ((0, 3, 0, dev_hp, dev_hm), (1, 1, 1, dev_hm, dev_hp)):
            j = slot_of(r, cc)
            copy = remote(
                f"comb{k}{i}", comb_s.at[i, span(k)], comb_r.at[i, span(k)], device
            )
            if not late and core != 1:
                sent.append(copy)

            def run():
                got(f"hop{k}{i}", hop_r.at[i, span(k)], source)
                total = part[j, span(k), :, half(cc)] + hop_r[i, span(k)].astype(F32)
                comb_s[i, span(k)] = total.astype(BF16)
                copy.start()

            if core is None:
                phase(late, j, run)
            else:
                pl.when((j != 3) & (c == core))(run)

    def finish(k, late):
        for cc, first, second in ((0, dev_hp, dev_hm), (1, dev_hm, dev_hp)):
            j = slot_of(0, cc)
            mine = pt.at[c, cc, span(k)]
            to_mate = remote(f"pt{k}{cc}", mine, mine, dev_mate)
            if not late:
                sent.append(to_mate)

            def run():
                got(f"dir{k}{1 - cc}", dir_r.at[1 - cc, span(k)], second)
                got(f"comb{k}{cc}", comb_r.at[cc, span(k)], first)
                pt[c, cc, span(k)] = part[j, span(k), :, half(cc)] + (
                    comb_r[cc, span(k)].astype(F32) + dir_r[1 - cc, span(k)].astype(F32)
                )
                to_mate.start()

            phase(late, j, run)

    compute(0, False)

    got("meta_far", meta_buf.at[1], dev_far)
    swap = meta_buf[0, 5:6, :] > 0.5
    for row, far_row in ((0, 4), (8, 12)):
        first = row // 2
        meta_all[c, first : first + 3, :] = meta_buf[0, row : row + 3, :]
        meta_all[c, first + 3 : first + 4, :] = jnp.where(
            swap, meta_buf[1, far_row : far_row + 1, :], meta_buf[0, row + 3 : row + 4, :]
        )
    send("meta_mate", meta_all.at[c], meta_all.at[c], dev_mate)

    b_got(1, 0)
    b_got(2, 0)
    far_line(0)
    compute(1, False)
    got("spare_p", relay.at[0], dev_xm)
    send("spare_pf", relay.at[0], spare.at[near], dev_xp)
    got("spare_m", relay.at[1], dev_xp)
    send("spare_mf", relay.at[1], spare.at[far], dev_xm)
    b_send(3)
    combine(0, False, 1)
    b_got(1, 1)
    b_got(2, 1)
    b_got(2, 2)
    b_got(1, 2)
    far_line(1)
    compute(2, False)
    combine(0, False, 0)
    combine(1, False)

    got("wzf_m", wbuf.at[2, u, v, :, lower], dev_hp)
    got("wzf_p", wbuf.at[2, u, v, :, upper], dev_hm)
    send("wu_p", w_at(u, v), w_at(u, v), dev_up)
    send("wu_m", w_at(u, v), w_at(u, v), dev_um)
    w_send(u, 0)
    own_w = []
    for p in range(4):
        for q in range(4):
            own_w.append(local(f"w{p}{q}", w_slice(p, q), wbuf.at[0, p, q]))

    got("spare_pf", spare.at[near], dev_xm)
    got("spare_mf", spare.at[far], dev_xp)
    own_a[3].wait()
    a_all[6 + c] = jnp.where(taking, spare[...], own3[...])
    send("mate_a3", a_all.at[6 + c], a_all.at[6 + c], dev_mate)
    got("mate_a3", a_all.at[7 - c], dev_mate)
    compute(0, True)
    compute(1, True)
    compute(2, True)
    combine(2, False)
    b_got(2, 3)
    b_got(1, 3)
    far_line(2)
    compute(3, False)
    compute(3, True)

    got("wu_p", w_at(um, v), dev_um)
    send(
        "wuf_p", wbuf.at[three, um, v, :, lower], wbuf.at[three, um, v, :, lower], dev_up
    )
    w_send(um, 1)
    got("wu_m", w_at(up, v), dev_up)
    send(
        "wuf_m", wbuf.at[three, up, v, :, upper], wbuf.at[three, up, v, :, upper], dev_um
    )
    w_send(up, 2)
    combine(0, True)
    combine(1, True)
    far_line(3)
    compute(4, False)
    compute(4, True)
    combine(2, True)
    combine(3, False)
    combine(3, True)
    got("wuf_p", wbuf.at[three, u2, v, :, lower], dev_um)
    got("wuf_m", wbuf.at[three, u2, v, :, upper], dev_up)
    w_send(u2, 3)
    got("wv_p0", w_at(u, vm), dev_vm)
    send("wvf_p0", w_at(u, vm), w_at(u, vm), dev_vp)
    got("wv_p1", w_at(um, vm), dev_vm)
    send("wvf_p1", w_at(um, vm), w_at(um, vm), dev_vp)
    combine(4, False)
    got("wv_m0", w_at(u, vp), dev_vp)
    got("wv_m1", w_at(um, vp), dev_vp)
    got("wv_m2", w_at(up, vp), dev_vp)
    send("wvf_m2", w_at(up, vp), w_at(up, vp), dev_vm)
    combine(4, True)
    got("wv_m3", w_at(u2, vp), dev_vp)
    send("wvf_m3", w_at(u2, vp), w_at(u2, vp), dev_vm)
    got("wv_p2", w_at(up, vm), dev_vm)
    got("wv_p3", w_at(u2, vm), dev_vm)
    for k in range(5):
        finish(k, False)
        finish(k, True)
    for k in range(5):
        for cc in range(2):
            got(f"pt{k}{cc}", pt.at[1 - c, cc, span(k)], dev_mate)

    def rank(there, here):
        step = (2 * ((there + 4 - here) % 4)) % 5
        return step - step // 4

    with scope("assemble"):
        for src in range(2):
            own = c == src
            u_src, v_src = jnp.where(own, u, v), jnp.where(own, v, u)
            for vv in range(4):
                kv = rank(vv, v_src)
                for uu in range(4):
                    ku = rank(uu, u_src)
                    place = jnp.where(kv == 3, 12 + ku, 3 + 2 * ku + kv)
                    place = jnp.where(kv == 0, ku, place)
                    for zz in range(2):
                        xx, yy = (uu, vv) if src == 0 else (vv, uu)
                        first = SHARE * (xx * 16 + zz * 8 + yy * 2 + src)
                        row = PADDED * zz
                        for cc in range(2):
                            ptd[first : first + SHARE, half(cc)] = pt[
                                src, cc, place, row : row + SHARE, :
                            ]
        for q in range(3):
            pth[q] = ptd[q * WCOLS : (q + 1) * WCOLS, :].astype(BF16)
        pth[3, :128] = jnp.zeros((128, 2 * BLOCK), BF16)
        pth[3, 128:] = ptd[3 * WCOLS :, :].astype(BF16)

    def screen(k, q):
        with scope(f"screen{k}"):

            @pl.loop(0, 2)
            def _(n):
                two = pl.ds(2 * n, 2)
                rows = pl.ds(pl.multiple_of(n * 8 * WROWS, 8 * WROWS), 8 * WROWS)
                value = jnp.dot(
                    wbuf[two, :, q].reshape(8 * WROWS, WCOLS),
                    pth[q],
                    preferred_element_type=F32,
                )
                if k == 0:
                    scr[rows, :] = value
                else:
                    scr[rows, :] += value

    for copy in own_w:
        copy.wait()
    screen(0, v)
    screen(1, vm)
    screen(2, vp)
    for tag in range(4):
        if tag < 2:
            got(f"wvf_p{tag}", w_at(around[tag], v2), dev_vm)
        else:
            got(f"wvf_m{tag}", w_at(around[tag], v2), dev_vp)
    screen(3, v2)
    with scope("bs"):
        for slot in range(2):
            total = jnp.zeros((BLOCK, BLOCK), F32)
            for rel in range(4):
                base = ((h + rel) % 4) * 736 + c * 368
                for skip, first, count in ((0, 0, 288), (304, 288, 80)):
                    total += lax.dot_general(
                        scr[pl.ds(rel * 4 * WROWS + skip, count), half(slot)],
                        ptd[pl.ds(pl.multiple_of(base + first, 16), count), half(slot)],
                        (((0,), (0,)), ((), ())),
                        preferred_element_type=F32,
                        precision=HIGHEST,
                    )
            bs_own[slot] = total
    send("bs", bs_own, bs_mate, dev_mate)

    got("meta_mate", meta_all.at[1 - c], dev_mate)
    with scope("places"):
        item = lax.broadcasted_iota(jnp.int32, (NB_SIGMA // 2, BLOCK), 0)
        rows = (item // 64) * 128 + (item // 8) % 2 * 64 + (item // 16) % 4 * 16 + c * 8 + item % 8
        rows = rows.astype(F32)
        columns = lax.broadcasted_iota(jnp.int32, (NB_SIGMA, BLOCK), 0).astype(F32)
        places = []
        for cc in range(2):
            j = slot_of(0, cc)
            index = meta_all[cc, pl.ds(j, 1), :]
            weight = meta_all[cc, pl.ds(4 + j, 1), :]
            places.append(((rows == index).astype(BF16), (columns == index).astype(BF16), weight))
    got("bs", bs_mate, dev_mate)
    with scope("spread"):
        spread = jnp.zeros((NB_SIGMA // 2, NB_SIGMA), F32)
        for slot in range(2):
            to_rows, to_columns, weight = places[slot]
            block = (bs_own[slot] + bs_mate[slot]) * weight
            high = block.astype(BF16)
            low = (block - high.astype(F32)).astype(BF16)
            for term in (high, low):
                wide = lax.dot_general(
                    term, to_columns, (((1,), (1,)), ((), ())), preferred_element_type=F32
                )
                spread += jnp.dot(to_rows, wide.astype(BF16), preferred_element_type=F32)
        plane_s[...] = spread.astype(BF16).reshape(4, 4, 16, NB_SIGMA)
    for (dx, dy), (place, device) in plane.items():
        send(f"plane{dx}{dy}", plane_s.at[place[0], place[1]], plane_r.at[x, y], device)
    total = plane_s[x, y].astype(F32)
    for dx, dy in plane:
        source = (x + 4 - dx) % 4, (y + 4 - dy) % 4
        landed = plane_r.at[source[0], source[1]]
        got(f"plane{dx}{dy}", landed, plane[(4 - dx) % 4, (4 - dy) % 4][1])
        total += landed[...].astype(F32)
    for zz in range(2):
        for hh in range(4):
            first = 8 * zz + 2 * hh
            line_s[zz, hh] = total[first : first + 2, :]
    for (dz, dh), (place, device) in line.items():
        send(f"line{dz}{dh}", line_s.at[place[0], place[1]], line_r.at[zl, h], device)
    result = line_s[zl, h]
    for dz, dh in line:
        source = (zl + dz) % 2, (h + 4 - dh) % 4
        landed = line_r.at[source[0], source[1]]
        got(f"line{dz}{dh}", landed, line[dz, (4 - dh) % 4][1])
        result += landed[...]
    out_ref[...] = result
    for copy in sent:
        copy.wait_send()
    for core in range(2):

        @pl.when(c == core)
        def _():
            for name, device in sent_by_core[core]:
                whole = core == 0 or name in ("by_p", "by_m")
                piece = b_at(0, 0) if whole else b_half(0, 0, 0)
                remote(name, piece, piece, device).wait_send()

    assert len(ids) <= N_COPIES


def per_device(pair_density, eigvecs, screening, occupation, window_start, window_len, slot_band):
    block, plane_rows = pair_density.shape[1:]
    eig = jnp.pad(eigvecs, ((0, PADDED - SHARE), (0, 0)))
    width = screening.shape[1]
    vmem = pl.BlockSpec(memory_space=pltpu.VMEM)
    hbm = pl.BlockSpec(memory_space=pltpu.HBM)
    scratch = [
        pltpu.VMEM((8, block, plane_rows), BF16),
        pltpu.VMEM((block, plane_rows), BF16),
        pltpu.VMEM((2, block // 2, plane_rows), BF16),
        pltpu.VMEM((block, plane_rows), BF16),
        pltpu.VMEM((16, 2, PADDED, plane_rows), BF16),
        pltpu.VMEM((4, 4, 4, WROWS, WCOLS), BF16),
        pltpu.VMEM((4, 16, PIECE, 2 * block), F32),
    ]
    scratch += [pltpu.VMEM((2, 16, PIECE, block), BF16)] * 6
    scratch += [
        pltpu.VMEM((2, 2, 16, PIECE, block), F32),
        pltpu.VMEM((width, 2 * block), F32),
        pltpu.VMEM((4, WCOLS, 2 * block), BF16),
        pltpu.VMEM((16 * WROWS, 2 * block), F32),
        pltpu.VMEM((2, 16, block), F32),
        pltpu.VMEM((2, 8, block), F32),
        pltpu.VMEM((2, block, block), F32),
        pltpu.VMEM((2, block, block), F32),
        pltpu.VMEM((4, 4, 16, NB_SIGMA), BF16),
        pltpu.VMEM((4, 4, 16, NB_SIGMA), BF16),
        pltpu.VMEM((2, 4, 2, NB_SIGMA), F32),
        pltpu.VMEM((2, 4, 2, NB_SIGMA), F32),
        pltpu.SemaphoreType.DMA((N_COPIES,)),
        pltpu.SemaphoreType.DMA((N_COPIES,)),
        pltpu.SemaphoreType.DMA((24,)),
    ]
    smem = pl.BlockSpec(memory_space=pltpu.SMEM)
    return pl.pallas_call(
        main_kernel,
        out_shape=jax.ShapeDtypeStruct((2, NB_SIGMA), F32),
        in_specs=[smem, smem, smem, vmem, hbm, hbm, hbm],
        out_specs=vmem,
        scratch_shapes=scratch,
        compiler_params=pltpu.CompilerParams(
            collective_id=0, has_side_effects=True, vmem_limit_bytes=60 * 1024 * 1024
        ),
        name="cohsex",
    )(
        window_start,
        window_len,
        slot_band,
        occupation.reshape(1, -1),
        pair_density,
        eig,
        screening,
    )


def solution(mesh):
    return jax.shard_map(
        per_device,
        mesh=mesh,
        in_specs=(
            P("band", None, "pw"),
            P("band", "pw"),
            P("pw", None),
            P(),
            P("band"),
            P("band"),
            P("band"),
        ),
        out_specs=P(("band", "pw"), None),
        check_vma=False,
    )
```

time: 143 us -> 124 us (0.87)
  Pallas kernels: 140 us -> 120 us
    pallas_call x1, Pallas kernels: 140 us -> 120 us  [per_device(): pl.pallas_call(main_kernel, out_shape=jax.ShapeDtypeStruct((2, NB_SIGMA),...]
where the time goes in v3:
time: 124 us; the launch traced here: 123 us
  Pallas kernels  120 us (97%)
  local copies, waits for them, and re-layouts  2.89 us (2%)
    pallas_call x1, Pallas kernels, per_device(): pl.pallas_call(main_kernel, out_shape=jax.ShapeDtypeStruct((2, NB_SIGMA),...  120 us

profile of v3, /device:TPU:1, one launch (start us, length us, event | category | flops | bytes accessed | tf_op | source)
XLA Modules:
  0.0 123.2 jit_solution(7825218814044434322)
XLA Ops:
  0.0 1.6 %pad.4.eig_ref = bf16[48,2304]{1,0:T(8,128)(2,1)} pad(bf16[46,2304]{1,0:T(8,128)(2,1)} %param.8, bf16[]{:T(256)} %constant.2.clone.1), padding=0_2x0_0 | pad | bytes 433154 | tf_op jit(solution)/shard_map/jit(_pad)/pad | solution.py:585
  1.6 120.3 %cohsex.1 = f32[2,512]{1,0:T(2,128)} custom-call(s32[5]{0:T(128)} %start_ref.1, s32[5]{0:T(128)} %len_ref.1, s32[5]{0:T(128)} %slot_ref.1, f32[1,128]{1,0:T(1,128)} %bitcast.1, bf16[5,128,2304]{2,1,0:T(8,128)(2,1)} %a_ref.1, bf16[48,2304]{1,0:T(8,128)(2,1)} %pad.4.eig_ref, bf16[736,2944]{1,0:T(8,128)(2,1)} %w_ref.1), custom_call_target="tpu_custom_call" | custom-call | tf_op jit(solution)/shard_map/cohsex/pallas_call | solution.py:617
  121.9 1.3 %copy.9 = f32[2,512]{1,0:T(2,128)} copy(f32[2,512]{1,0:T(2,128)} %cohsex.1) | data formatting | bytes 8192

commit v4 on v3

--- a/solution.py
+++ b/solution.py
@@ -12,7 +12,7 @@
 HIGHEST = lax.Precision.HIGHEST
 SHARE, PADDED = 46, 48
 PIECE = 2 * PADDED
-CHUNKS = ((0, 4), (4, 6), (6, 10), (10, 12), (12, 16))
+CHUNKS = ((0, 4), (4, 6), (6, 8), (8, 10), (10, 12), (12, 16))
 
 
 def place_of(kv, ku):
@@ -22,7 +22,7 @@
 
 
 WROWS, WCOLS = 96, 768
-N_COPIES = 200
+N_COPIES = 220
 scope = jax.named_scope
 
 
@@ -39,6 +39,7 @@
     spare,
     relay,
     own3,
+    share,
     bbuf,
     wbuf,
     part,
@@ -51,7 +52,10 @@
     pt,
     ptd,
     pth,
-    scr,
+    ptd_h,
+    ptd_l,
+    scr_h,
+    scr_l,
     meta_buf,
     meta_all,
     bs_own,
@@ -102,10 +106,12 @@
                 place = ((zl + dz) % 2, (h + dh) % 4)
                 line[dz, dh] = place, (x * 16 + place[0] * 8 + y * 2 + c, place[1])
     dev_xp, dev_xm = plane[1, 0][1], plane[3, 0][1]
-    peers = [dev_mate] + [device for _, device in [*plane.values(), *line.values()]]
+    peers = [dev_mate, dev_up, dev_um, dev_vp, dev_vm, dev_hp, dev_hm, dev_zl, dev_far]
     for peer in peers:
         pl.semaphore_signal(barrier, inc=1, device_id=peer, device_id_type=pl.DeviceIdType.MESH)
 
+    own_b = pltpu.make_async_copy(eig_ref, share, lsem.at[23])
+    own_b.start()
     lane = lax.broadcasted_iota(jnp.int32, (1, BLOCK), 1)
     for j in range(5):
         kept = (lane < len_ref[j]) & (slot_ref[j] >= 0)
@@ -114,12 +120,16 @@
         meta_buf[0, 8 + j : 9 + j, :] = jnp.broadcast_to(0.5 - value, (1, BLOCK))
     taking = slot_ref[3] < 0
     meta_buf[0, 5:6, :] = jnp.where(taking, 1.0, 0.0) + jnp.zeros((1, BLOCK), F32)
+    own_b.wait()
+    bbuf[0, zl, :SHARE] = share[...]
+    bbuf[0, zl, SHARE:] = jnp.zeros((PADDED - SHARE, share.shape[1]), BF16)
     with scope('barrier'):
         pl.semaphore_wait(barrier, len(peers))
 
     ids = {}
     sent = []
     sent_by_core = ([], [])
+    pieces = {}
 
     def remote(name, src, dst, device):
         i = ids.setdefault(name, len(ids))
@@ -175,8 +185,9 @@
         send(f"wv_m{tag}", w_at(uu, v), w_at(uu, v), dev_vm)
 
     def b_send(ku):
-        send(f"bv_p{ku}", b_at(0, ku), b_at(1, ku), dev_vp)
-        send(f"bv_m{ku}", b_at(0, ku), b_at(2, ku), dev_vm)
+        for name, kv, device in ((f"bv_p{ku}", 1, dev_vp), (f"bv_m{ku}", 2, dev_vm)):
+            remote(name, b_at(0, ku), b_at(kv, ku), device).start()
+            pieces[name] = device
 
     def b_got(kv, ku):
         if ku:
@@ -186,12 +197,12 @@
                 device = dev_vm if kv == 1 else dev_vp
                 got(f"bv_{'pm'[kv - 1]}0{tag}", b_half(kv, 0, zz), device)
 
-    def far_line(step):
+    def far_line(step, core=None):
         def core0():
-            for kv, ku in (((1, 0),), ((1, 1), (2, 2)), ((2, 3),), ())[step]:
+            for kv, ku in (((1, 0),), ((1, 1),), ((2, 2),), ((2, 3),), ())[step]:
                 device = dev_vp if kv == 1 else dev_vm
                 send(f"bf{kv}{ku}", b_at(kv, ku), b_at(3, ku), device, sent_by_core[0])
-            if step == 3:
+            if step == 4:
                 for ku in range(4):
                     got(f"bf{1 if ku < 2 else 2}{ku}", b_at(3, ku), dev_vm if ku < 2 else dev_vp)
 
@@ -201,11 +212,13 @@
                 send("bx_p", b_half(1, 0, zl), b_half(3, 0, zl), dev_vp, into)
                 send("bx_m", b_half(2, 0, oz), b_half(3, 0, oz), dev_vm, into)
             elif step == 1:
+                pass
+            elif step == 2:
                 got("bx_p", b_half(3, 0, zl), dev_vm)
                 got("bx_m", b_half(3, 0, oz), dev_vp)
                 send("by_p", b_at(3, 0), b_at(3, 1), dev_up, into)
                 send("by_m", b_at(3, 0), b_at(3, 2), dev_um, into)
-            elif step == 2:
+            elif step == 3:
                 got("by_p", b_at(3, 1), dev_um)
                 send("byf_p", b_half(3, 1, zl), b_half(3, 3, zl), dev_up, into)
                 got("by_m", b_at(3, 2), dev_up)
@@ -214,21 +227,22 @@
                 got("byf_p", b_half(3, 3, zl), dev_um)
                 got("byf_m", b_half(3, 3, oz), dev_up)
 
-        pl.when(c == 0)(core0)
-        pl.when(c == 1)(core1)
-
-    send("zl", eig_ref, b_half(0, 0, zl), dev_zl)
-    own_b = local("b", eig_ref, b_half(0, 0, zl))
-    send("bu_p0", eig_ref, b_half(0, 1, zl), dev_up)
-    send("bu_m0", eig_ref, b_half(0, 2, zl), dev_um)
+        if core != 1:
+            pl.when(c == 0)(core0)
+        if core != 0:
+            pl.when(c == 1)(core1)
+
+    send("zl", b_half(0, 0, zl), b_half(0, 0, zl), dev_zl)
+    send("bu_p0", b_half(0, 0, zl), b_half(0, 1, zl), dev_up)
+    send("bu_m0", b_half(0, 0, zl), b_half(0, 2, zl), dev_um)
     send("meta_far", meta_buf.at[0], meta_buf.at[1], dev_far)
     own_a = []
     for j in range(3):
         own_a.append(local(f"a{j}", a_ref.at[j], a_all.at[2 * j + c]))
         send(f"mate_a{j}", a_ref.at[j], a_all.at[2 * j + c], dev_mate)
     own_a.append(local("a3", a_ref.at[3], own3))
-    send("bv_p0a", eig_ref, b_half(1, 0, zl), dev_vp)
-    send("bv_m0a", eig_ref, b_half(2, 0, zl), dev_vm)
+    send("bv_p0a", b_half(0, 0, zl), b_half(1, 0, zl), dev_vp)
+    send("bv_m0a", b_half(0, 0, zl), b_half(2, 0, zl), dev_vm)
 
     got("zl", b_half(0, 0, oz), dev_zl)
     send("bu_p1", b_half(0, 0, oz), b_half(0, 1, oz), dev_up)
@@ -248,12 +262,11 @@
     send("spare_m", a_ref.at[4, far], relay.at[1], dev_xm)
     got("bu_p1", b_half(0, 1, oz), dev_um)
     b_send(1)
-    b_send(2)
+    pl.when(c == 0)(lambda: b_send(2))
     got("wz_m", wbuf.at[1, u, v], dev_hp)
     send("wzf_m", wbuf.at[1, u, v, :, lower], wbuf.at[2, u, v, :, lower], dev_hm)
     got("wz_p", wbuf.at[3, u, v], dev_hm)
     send("wzf_p", wbuf.at[3, u, v, :, upper], wbuf.at[2, u, v, :, upper], dev_hp)
-    own_b.wait()
     for j in range(3):
         own_a[j].wait()
         got(f"mate_a{j}", a_all.at[2 * j + 1 - c], dev_mate)
@@ -278,6 +291,8 @@
 
     def span(k):
         return pl.ds(CHUNKS[k][0], CHUNKS[k][1] - CHUNKS[k][0])
+
+    chunks_sent = {}
 
     def phase(late, j, run):
         pl.when((j == 3) if late else (j != 3))(run)
@@ -302,8 +317,7 @@
                 copy = remote(
                     f"{name}{k}{i}", send_buf.at[i, span(k)], recv_buf.at[i, span(k)], device
                 )
-                if not late:
-                    sent.append(copy)
+                chunks_sent[f"{name}{k}{i}"] = (f"{name}{k}{i}", k, i, device)
 
                 def run():
                     send_buf[i, span(k)] = part[j, span(k), :, half(cc)].astype(BF16)
@@ -317,8 +331,7 @@
             copy = remote(
                 f"comb{k}{i}", comb_s.at[i, span(k)], comb_r.at[i, span(k)], device
             )
-            if not late and core != 1:
-                sent.append(copy)
+            chunks_sent[f"comb{k}{i}"] = (f"comb{k}{i}", k, i, device)
 
             def run():
                 got(f"hop{k}{i}", hop_r.at[i, span(k)], source)
@@ -369,22 +382,35 @@
     send("spare_pf", relay.at[0], spare.at[near], dev_xp)
     got("spare_m", relay.at[1], dev_xp)
     send("spare_mf", relay.at[1], spare.at[far], dev_xm)
+    pl.when(c == 1)(lambda: b_send(2))
     b_send(3)
     combine(0, False, 1)
     b_got(1, 1)
+    far_line(1)
     b_got(2, 1)
+    compute(2, False)
+    combine(0, False, 0)
     b_got(2, 2)
     b_got(1, 2)
-    far_line(1)
-    compute(2, False)
-    combine(0, False, 0)
+    far_line(2)
+    compute(3, False)
     combine(1, False)
+
+    def fifth(core):
+        b_got(2, 3)
+        far_line(3, core)
+        b_got(1, 3)
+        compute(4, False)
+
+    @pl.when(c == 0)
+    def _():
+        fifth(0)
+        combine(2, False)
 
     got("wzf_m", wbuf.at[2, u, v, :, lower], dev_hp)
     got("wzf_p", wbuf.at[2, u, v, :, upper], dev_hm)
     send("wu_p", w_at(u, v), w_at(u, v), dev_up)
     send("wu_m", w_at(u, v), w_at(u, v), dev_um)
-    w_send(u, 0)
     own_w = []
     for p in range(4):
         for q in range(4):
@@ -396,15 +422,13 @@
     a_all[6 + c] = jnp.where(taking, spare[...], own3[...])
     send("mate_a3", a_all.at[6 + c], a_all.at[6 + c], dev_mate)
     got("mate_a3", a_all.at[7 - c], dev_mate)
-    compute(0, True)
-    compute(1, True)
-    compute(2, True)
-    combine(2, False)
-    b_got(2, 3)
-    b_got(1, 3)
-    far_line(2)
-    compute(3, False)
-    compute(3, True)
+    for k in range(4):
+        compute(k, True)
+    combine(2, False, 1)
+    combine(3, False)
+    pl.when(c == 1)(lambda: fifth(1))
+    w_send(u, 0)
+    compute(4, True)
 
     got("wu_p", w_at(um, v), dev_um)
     send(
@@ -418,12 +442,13 @@
     w_send(up, 2)
     combine(0, True)
     combine(1, True)
-    far_line(3)
-    compute(4, False)
-    compute(4, True)
+    far_line(4)
+    compute(5, False)
+    compute(5, True)
     combine(2, True)
-    combine(3, False)
     combine(3, True)
+    combine(4, False)
+    combine(4, True)
     got("wuf_p", wbuf.at[three, u2, v, :, lower], dev_um)
     got("wuf_m", wbuf.at[three, u2, v, :, upper], dev_up)
     w_send(u2, 3)
@@ -431,20 +456,20 @@
     send("wvf_p0", w_at(u, vm), w_at(u, vm), dev_vp)
     got("wv_p1", w_at(um, vm), dev_vm)
     send("wvf_p1", w_at(um, vm), w_at(um, vm), dev_vp)
-    combine(4, False)
+    combine(5, False)
     got("wv_m0", w_at(u, vp), dev_vp)
     got("wv_m1", w_at(um, vp), dev_vp)
     got("wv_m2", w_at(up, vp), dev_vp)
     send("wvf_m2", w_at(up, vp), w_at(up, vp), dev_vm)
-    combine(4, True)
+    combine(5, True)
     got("wv_m3", w_at(u2, vp), dev_vp)
     send("wvf_m3", w_at(u2, vp), w_at(u2, vp), dev_vm)
     got("wv_p2", w_at(up, vm), dev_vm)
     got("wv_p3", w_at(u2, vm), dev_vm)
-    for k in range(5):
+    for k in range(6):
         finish(k, False)
         finish(k, True)
-    for k in range(5):
+    for k in range(6):
         for cc in range(2):
             got(f"pt{k}{cc}", pt.at[1 - c, cc, span(k)], dev_mate)
 
@@ -470,52 +495,52 @@
                             ptd[first : first + SHARE, half(cc)] = pt[
                                 src, cc, place, row : row + SHARE, :
                             ]
+        high = ptd[...].astype(BF16)
+        ptd_h[...] = high
+        ptd_l[...] = (ptd[...] - high.astype(F32)).astype(BF16)
         for q in range(3):
-            pth[q] = ptd[q * WCOLS : (q + 1) * WCOLS, :].astype(BF16)
+            pth[q] = high[q * WCOLS : (q + 1) * WCOLS, :]
         pth[3, :128] = jnp.zeros((128, 2 * BLOCK), BF16)
-        pth[3, 128:] = ptd[3 * WCOLS :, :].astype(BF16)
-
-    def screen(k, q):
-        with scope(f"screen{k}"):
-
-            @pl.loop(0, 2)
-            def _(n):
-                two = pl.ds(2 * n, 2)
-                rows = pl.ds(pl.multiple_of(n * 8 * WROWS, 8 * WROWS), 8 * WROWS)
-                value = jnp.dot(
-                    wbuf[two, :, q].reshape(8 * WROWS, WCOLS),
-                    pth[q],
-                    preferred_element_type=F32,
-                )
-                if k == 0:
-                    scr[rows, :] = value
-                else:
-                    scr[rows, :] += value
+        pth[3, 128:] = high[3 * WCOLS :, :]
 
     for copy in own_w:
         copy.wait()
-    screen(0, v)
-    screen(1, vm)
-    screen(2, vp)
     for tag in range(4):
         if tag < 2:
             got(f"wvf_p{tag}", w_at(around[tag], v2), dev_vm)
         else:
             got(f"wvf_m{tag}", w_at(around[tag], v2), dev_vp)
-    screen(3, v2)
+    with scope("screen"):
+
+        @pl.loop(0, 4)
+        def _(rel):
+            value = jnp.zeros((4 * WROWS, 2 * BLOCK), F32)
+            for q in range(4):
+                value += jnp.dot(
+                    wbuf[rel, :, q].reshape(4 * WROWS, WCOLS),
+                    pth[q],
+                    preferred_element_type=F32,
+                )
+            rows = pl.ds(pl.multiple_of(rel * 4 * WROWS, 4 * WROWS), 4 * WROWS)
+            high = value.astype(BF16)
+            scr_h[rows, :] = high
+            scr_l[rows, :] = (value - high.astype(F32)).astype(BF16)
+
     with scope("bs"):
         for slot in range(2):
             total = jnp.zeros((BLOCK, BLOCK), F32)
             for rel in range(4):
                 base = ((h + rel) % 4) * 736 + c * 368
                 for skip, first, count in ((0, 0, 288), (304, 288, 80)):
-                    total += lax.dot_general(
-                        scr[pl.ds(rel * 4 * WROWS + skip, count), half(slot)],
-                        ptd[pl.ds(pl.multiple_of(base + first, 16), count), half(slot)],
-                        (((0,), (0,)), ((), ())),
-                        preferred_element_type=F32,
-                        precision=HIGHEST,
-                    )
+                    left_rows = pl.ds(rel * 4 * WROWS + skip, count)
+                    right_rows = pl.ds(pl.multiple_of(base + first, 16), count)
+                    for left, right in ((scr_h, ptd_h), (scr_h, ptd_l), (scr_l, ptd_h)):
+                        total += lax.dot_general(
+                            left[left_rows, half(slot)],
+                            right[right_rows, half(slot)],
+                            (((0,), (0,)), ((), ())),
+                            preferred_element_type=F32,
+                        )
             bs_own[slot] = total
     send("bs", bs_own, bs_mate, dev_mate)
 
@@ -568,6 +593,11 @@
     out_ref[...] = result
     for copy in sent:
         copy.wait_send()
+    for name, device in pieces.items():
+        remote(name, b_at(0, 0), b_at(0, 0), device).wait_send()
+    for name, k, i, device in chunks_sent.values():
+        piece = hop_s.at[i, span(k)]
+        remote(name, piece, piece, device).wait_send()
     for core in range(2):
 
         @pl.when(c == core)
@@ -582,7 +612,6 @@
 
 def per_device(pair_density, eigvecs, screening, occupation, window_start, window_len, slot_band):
     block, plane_rows = pair_density.shape[1:]
-    eig = jnp.pad(eigvecs, ((0, PADDED - SHARE), (0, 0)))
     width = screening.shape[1]
     vmem = pl.BlockSpec(memory_space=pltpu.VMEM)
     hbm = pl.BlockSpec(memory_space=pltpu.HBM)
@@ -591,6 +620,7 @@
         pltpu.VMEM((block, plane_rows), BF16),
         pltpu.VMEM((2, block // 2, plane_rows), BF16),
         pltpu.VMEM((block, plane_rows), BF16),
+        pltpu.VMEM((SHARE, plane_rows), BF16),
         pltpu.VMEM((16, 2, PADDED, plane_rows), BF16),
         pltpu.VMEM((4, 4, 4, WROWS, WCOLS), BF16),
         pltpu.VMEM((4, 16, PIECE, 2 * block), F32),
@@ -600,7 +630,10 @@
         pltpu.VMEM((2, 2, 16, PIECE, block), F32),
         pltpu.VMEM((width, 2 * block), F32),
         pltpu.VMEM((4, WCOLS, 2 * block), BF16),
-        pltpu.VMEM((16 * WROWS, 2 * block), F32),
+        pltpu.VMEM((width, 2 * block), BF16),
+        pltpu.VMEM((width, 2 * block), BF16),
+        pltpu.VMEM((16 * WROWS, 2 * block), BF16),
+        pltpu.VMEM((16 * WROWS, 2 * block), BF16),
         pltpu.VMEM((2, 16, block), F32),
         pltpu.VMEM((2, 8, block), F32),
         pltpu.VMEM((2, block, block), F32),
@@ -630,7 +663,7 @@
         slot_band,
         occupation.reshape(1, -1),
         pair_density,
-        eig,
+        eigvecs,
         screening,
     )
 

time: 124 us -> 120 us (0.968)
  Pallas kernels: 120 us -> 118 us
  local copies, waits for them, and re-layouts: 2.89 us -> 1.28 us
    pallas_call x1, Pallas kernels: 120 us -> 118 us  [per_device(): pl.pallas_call(main_kernel, out_shape=jax.ShapeDtypeStruct((2, NB_SIGMA),...]
    pad x1 -> x0, local copies, waits for them, and re-layouts: 1.62 us -> none  [per_device(): eig = jnp.pad(eigvecs, ((0, PADDED - SHARE), (0, 0)))]
where the time goes in v4:
time: 120 us; the launch traced here: 119 us
  Pallas kernels  118 us (98%)
  local copies, waits for them, and re-layouts  1.28 us (1%)
    pallas_call x1, Pallas kernels, per_device(): pl.pallas_call(main_kernel, out_shape=jax.ShapeDtypeStruct((2, NB_SIGMA),...  118 us

profile of v4, /device:TPU:1, one launch (start us, length us, event | category | flops | bytes accessed | tf_op | source)
XLA Modules:
  0.0 118.9 jit_solution(1432223380988037263)
XLA Ops:
  0.0 117.6 %cohsex.1 = f32[2,512]{1,0:T(2,128)} custom-call(s32[5]{0:T(128)} %start_ref.1, s32[5]{0:T(128)} %len_ref.1, s32[5]{0:T(128)} %slot_ref.1, f32[1,128]{1,0:T(1,128)} %bitcast.1, bf16[5,128,2304]{2,1,0:T(8,128)(2,1)} %a_ref.1, bf16[46,2304]{1,0:T(8,128)(2,1)} %eig_ref.1, bf16[736,2944]{1,0:T(8,128)(2,1)} %w_ref.1), custom_call_target="tpu_custom_call" | custom-call | tf_op jit(solution)/shard_map/cohsex/pallas_call | solution.py:650
  117.6 1.3 %copy.9 = f32[2,512]{1,0:T(2,128)} copy(f32[2,512]{1,0:T(2,128)} %cohsex.1) | data formatting | bytes 8192

commit v5 on v4

--- a/solution.py
+++ b/solution.py
@@ -22,7 +22,7 @@
 
 
 WROWS, WCOLS = 96, 768
-N_COPIES = 220
+N_COPIES = 280
 scope = jax.named_scope
 
 
@@ -54,6 +54,7 @@
     pth,
     ptd_h,
     ptd_l,
+    scr,
     scr_h,
     scr_l,
     meta_buf,
@@ -120,6 +121,9 @@
         meta_buf[0, 8 + j : 9 + j, :] = jnp.broadcast_to(0.5 - value, (1, BLOCK))
     taking = slot_ref[3] < 0
     meta_buf[0, 5:6, :] = jnp.where(taking, 1.0, 0.0) + jnp.zeros((1, BLOCK), F32)
+    for rel in range(1, 4):
+        for p in range(4):
+            wbuf[rel, p, 3, :, :128] = jnp.zeros((WROWS, 128), BF16)
     own_b.wait()
     bbuf[0, zl, :SHARE] = share[...]
     bbuf[0, zl, SHARE:] = jnp.zeros((PADDED - SHARE, share.shape[1]), BF16)
@@ -169,20 +173,67 @@
     def b_at(kv, ku):
         return bbuf.at[place_of(kv, ku)]
 
-    three = pl.ds(1, 3)
-    lower, upper = pl.ds(0, WCOLS // 2), pl.ds(WCOLS // 2, WCOLS // 2)
+    kinds = {"full": (128, 640), "lower": (128, 256), "upper": (384, 384)}
+
+    def w_copies(kind, p, q):
+        lanes = kinds[kind]
+        yield "a", (16, WROWS - 16), lanes, None
+        yield "b", (0, 16), lanes, p != 3
+        if kind != "upper":
+            yield "c", (0, WROWS), (0, 128), q != 3
+
+    def guarded(needed, run):
+        if needed is None:
+            run()
+        else:
+            pl.when(needed)(run)
+
+    def w_own(p, q):
+        def view(rows, lanes):
+            row = pl.multiple_of(c * 368 + p * WROWS - 16 * (p // 3) + rows[0], 16)
+            col = pl.multiple_of(q * WCOLS - 128 * (q // 3) + lanes[0], 128)
+            return w_ref.at[pl.ds(row, rows[1]), pl.ds(col, lanes[1])]
+
+        return view
+
+    def w_one(rel):
+        return lambda rows, lanes: wbuf.at[rel, u, v, pl.ds(*rows), pl.ds(*lanes)]
 
     def w_at(uu, vv):
-        return wbuf.at[three, uu, vv]
-
-    def w_slice(p, q):
-        row = pl.multiple_of(c * 368 + p * WROWS - 16 * (p // 3), 16)
-        col = pl.multiple_of(q * WCOLS - 128 * (q // 3), 128)
-        return w_ref.at[pl.ds(row, WROWS), pl.ds(col, WCOLS)]
+        return lambda rows, lanes: wbuf.at[pl.ds(1, 3), uu, vv, pl.ds(*rows), pl.ds(*lanes)]
+
+    w_sent = []
+
+    def w_move(name, src, dst, device, p, q, kind="full"):
+        for tag, rows, lanes, needed in w_copies(kind, p, q):
+            guarded(
+                needed,
+                lambda: remote(name + tag, src(rows, lanes), dst(rows, lanes), device).start(),
+            )
+        w_sent.append((name, src, device, p, q, kind))
+
+    def w_got(name, landing, device, p, q, kind="full"):
+        with scope("got_" + name):
+            for tag, rows, lanes, needed in w_copies(kind, p, q):
+
+                def run():
+                    here = landing(rows, lanes)
+                    remote(name + tag, here, here, device).wait_recv()
+
+                guarded(needed, run)
+
+    def w_left(name, src, device, p, q, kind):
+        for tag, rows, lanes, needed in w_copies(kind, p, q):
+
+            def run():
+                here = src(rows, lanes)
+                remote(name + tag, here, here, device).wait_send()
+
+            guarded(needed, run)
 
     def w_send(uu, tag):
-        send(f"wv_p{tag}", w_at(uu, v), w_at(uu, v), dev_vp)
-        send(f"wv_m{tag}", w_at(uu, v), w_at(uu, v), dev_vm)
+        w_move(f"wv_p{tag}", w_at(uu, v), w_at(uu, v), dev_vp, uu, v)
+        w_move(f"wv_m{tag}", w_at(uu, v), w_at(uu, v), dev_vm, uu, v)
 
     def b_send(ku):
         for name, kv, device in ((f"bv_p{ku}", 1, dev_vp), (f"bv_m{ku}", 2, dev_vm)):
@@ -249,8 +300,8 @@
     send("bu_m1", b_half(0, 0, oz), b_half(0, 2, oz), dev_um)
     send("bv_p0b", b_half(0, 0, oz), b_half(1, 0, oz), dev_vp)
     send("bv_m0b", b_half(0, 0, oz), b_half(2, 0, oz), dev_vm)
-    send("wz_m", w_slice(u, v), wbuf.at[1, u, v], dev_hm)
-    send("wz_p", w_slice(u, v), wbuf.at[3, u, v], dev_hp)
+    w_move("wz_m", w_own(u, v), w_one(1), dev_hm, u, v)
+    w_move("wz_p", w_own(u, v), w_one(3), dev_hp, u, v)
 
     got("bu_p0", b_half(0, 1, zl), dev_um)
     send("buf_p", b_half(0, 1, zl), b_half(0, 3, zl), dev_up)
@@ -263,10 +314,10 @@
     got("bu_p1", b_half(0, 1, oz), dev_um)
     b_send(1)
     pl.when(c == 0)(lambda: b_send(2))
-    got("wz_m", wbuf.at[1, u, v], dev_hp)
-    send("wzf_m", wbuf.at[1, u, v, :, lower], wbuf.at[2, u, v, :, lower], dev_hm)
-    got("wz_p", wbuf.at[3, u, v], dev_hm)
-    send("wzf_p", wbuf.at[3, u, v, :, upper], wbuf.at[2, u, v, :, upper], dev_hp)
+    w_got("wz_m", w_one(1), dev_hp, u, v)
+    w_move("wzf_m", w_one(1), w_one(2), dev_hm, u, v, "lower")
+    w_got("wz_p", w_one(3), dev_hm, u, v)
+    w_move("wzf_p", w_one(3), w_one(2), dev_hp, u, v, "upper")
     for j in range(3):
         own_a[j].wait()
         got(f"mate_a{j}", a_all.at[2 * j + 1 - c], dev_mate)
@@ -390,56 +441,71 @@
     b_got(2, 1)
     compute(2, False)
     combine(0, False, 0)
-    b_got(2, 2)
-    b_got(1, 2)
-    far_line(2)
-    compute(3, False)
-    combine(1, False)
+    far_line(2, 1)
+
+    def fourth():
+        b_got(2, 2)
+        b_got(1, 2)
+        compute(3, False)
 
     def fifth(core):
         b_got(2, 3)
-        far_line(3, core)
+        if core == 0:
+            far_line(3, 0)
         b_got(1, 3)
         compute(4, False)
 
     @pl.when(c == 0)
     def _():
-        fifth(0)
-        combine(2, False)
-
-    got("wzf_m", wbuf.at[2, u, v, :, lower], dev_hp)
-    got("wzf_p", wbuf.at[2, u, v, :, upper], dev_hm)
-    send("wu_p", w_at(u, v), w_at(u, v), dev_up)
-    send("wu_m", w_at(u, v), w_at(u, v), dev_um)
-    own_w = []
-    for p in range(4):
-        for q in range(4):
-            own_w.append(local(f"w{p}{q}", w_slice(p, q), wbuf.at[0, p, q]))
+        b_got(2, 2)
+        far_line(2, 0)
+        b_got(1, 2)
+        compute(3, False)
+        combine(1, False, 0)
 
     got("spare_pf", spare.at[near], dev_xm)
     got("spare_mf", spare.at[far], dev_xp)
     own_a[3].wait()
     a_all[6 + c] = jnp.where(taking, spare[...], own3[...])
     send("mate_a3", a_all.at[6 + c], a_all.at[6 + c], dev_mate)
+
+    @pl.when(c == 0)
+    def _():
+        fifth(0)
+        combine(2, False, 0)
+
+    combine(1, False, 1)
     got("mate_a3", a_all.at[7 - c], dev_mate)
-    for k in range(4):
+    for k in range(3):
         compute(k, True)
+
+    w_got("wzf_m", w_one(2), dev_hp, u, v, "lower")
+    w_got("wzf_p", w_one(2), dev_hm, u, v, "upper")
+    w_move("wu_p", w_at(u, v), w_at(u, v), dev_up, u, v)
+    w_move("wu_m", w_at(u, v), w_at(u, v), dev_um, u, v)
+    own_w = []
+    for p in range(4):
+        for q in range(4):
+            own_w.append(local(f"w{p}{q}", w_own(p, q)((0, WROWS), (0, WCOLS)), wbuf.at[0, p, q]))
     combine(2, False, 1)
-    combine(3, False)
-    pl.when(c == 1)(lambda: fifth(1))
+
+    @pl.when(c == 1)
+    def _():
+        fourth()
+        far_line(3, 1)
+        fifth(1)
+
+    compute(3, True)
     w_send(u, 0)
     compute(4, True)
 
-    got("wu_p", w_at(um, v), dev_um)
-    send(
-        "wuf_p", wbuf.at[three, um, v, :, lower], wbuf.at[three, um, v, :, lower], dev_up
-    )
+    w_got("wu_p", w_at(um, v), dev_um, um, v)
+    w_move("wuf_p", w_at(um, v), w_at(um, v), dev_up, um, v, "lower")
     w_send(um, 1)
-    got("wu_m", w_at(up, v), dev_up)
-    send(
-        "wuf_m", wbuf.at[three, up, v, :, upper], wbuf.at[three, up, v, :, upper], dev_um
-    )
+    w_got("wu_m", w_at(up, v), dev_up, up, v)
+    w_move("wuf_m", w_at(up, v), w_at(up, v), dev_um, up, v, "upper")
     w_send(up, 2)
+    combine(3, False)
     combine(0, True)
     combine(1, True)
     far_line(4)
@@ -449,23 +515,23 @@
     combine(3, True)
     combine(4, False)
     combine(4, True)
-    got("wuf_p", wbuf.at[three, u2, v, :, lower], dev_um)
-    got("wuf_m", wbuf.at[three, u2, v, :, upper], dev_up)
+    w_got("wuf_p", w_at(u2, v), dev_um, u2, v, "lower")
+    w_got("wuf_m", w_at(u2, v), dev_up, u2, v, "upper")
     w_send(u2, 3)
-    got("wv_p0", w_at(u, vm), dev_vm)
-    send("wvf_p0", w_at(u, vm), w_at(u, vm), dev_vp)
-    got("wv_p1", w_at(um, vm), dev_vm)
-    send("wvf_p1", w_at(um, vm), w_at(um, vm), dev_vp)
+    w_got("wv_p0", w_at(u, vm), dev_vm, u, vm)
+    w_move("wvf_p0", w_at(u, vm), w_at(u, vm), dev_vp, u, vm)
+    w_got("wv_p1", w_at(um, vm), dev_vm, um, vm)
+    w_move("wvf_p1", w_at(um, vm), w_at(um, vm), dev_vp, um, vm)
     combine(5, False)
-    got("wv_m0", w_at(u, vp), dev_vp)
-    got("wv_m1", w_at(um, vp), dev_vp)
-    got("wv_m2", w_at(up, vp), dev_vp)
-    send("wvf_m2", w_at(up, vp), w_at(up, vp), dev_vm)
+    w_got("wv_m0", w_at(u, vp), dev_vp, u, vp)
+    w_got("wv_m1", w_at(um, vp), dev_vp, um, vp)
+    w_got("wv_m2", w_at(up, vp), dev_vp, up, vp)
+    w_move("wvf_m2", w_at(up, vp), w_at(up, vp), dev_vm, up, vp)
     combine(5, True)
-    got("wv_m3", w_at(u2, vp), dev_vp)
-    send("wvf_m3", w_at(u2, vp), w_at(u2, vp), dev_vm)
-    got("wv_p2", w_at(up, vm), dev_vm)
-    got("wv_p3", w_at(u2, vm), dev_vm)
+    w_got("wv_m3", w_at(u2, vp), dev_vp, u2, vp)
+    w_move("wvf_m3", w_at(u2, vp), w_at(u2, vp), dev_vm, u2, vp)
+    w_got("wv_p2", w_at(up, vm), dev_vm, up, vm)
+    w_got("wv_p3", w_at(u2, vm), dev_vm, u2, vm)
     for k in range(6):
         finish(k, False)
         finish(k, True)
@@ -505,26 +571,34 @@
 
     for copy in own_w:
         copy.wait()
+
+    def screened(rel, q):
+        return jnp.dot(
+            wbuf[rel, :, q].reshape(4 * WROWS, WCOLS), pth[q], preferred_element_type=F32
+        )
+
+    def rows_of(rel):
+        return pl.ds(pl.multiple_of(rel * 4 * WROWS, 4 * WROWS), 4 * WROWS)
+
+    with scope("screen"):
+
+        @pl.loop(0, 4)
+        def _(rel):
+            scr[rows_of(rel), :] = screened(rel, v) + screened(rel, vm) + screened(rel, vp)
+
     for tag in range(4):
         if tag < 2:
-            got(f"wvf_p{tag}", w_at(around[tag], v2), dev_vm)
+            w_got(f"wvf_p{tag}", w_at(around[tag], v2), dev_vm, around[tag], v2)
         else:
-            got(f"wvf_m{tag}", w_at(around[tag], v2), dev_vp)
-    with scope("screen"):
+            w_got(f"wvf_m{tag}", w_at(around[tag], v2), dev_vp, around[tag], v2)
+    with scope("screen_last"):
 
         @pl.loop(0, 4)
         def _(rel):
-            value = jnp.zeros((4 * WROWS, 2 * BLOCK), F32)
-            for q in range(4):
-                value += jnp.dot(
-                    wbuf[rel, :, q].reshape(4 * WROWS, WCOLS),
-                    pth[q],
-                    preferred_element_type=F32,
-                )
-            rows = pl.ds(pl.multiple_of(rel * 4 * WROWS, 4 * WROWS), 4 * WROWS)
+            value = scr[rows_of(rel), :] + screened(rel, v2)
             high = value.astype(BF16)
-            scr_h[rows, :] = high
-            scr_l[rows, :] = (value - high.astype(F32)).astype(BF16)
+            scr_h[rows_of(rel), :] = high
+            scr_l[rows_of(rel), :] = (value - high.astype(F32)).astype(BF16)
 
     with scope("bs"):
         for slot in range(2):
@@ -593,6 +667,8 @@
     out_ref[...] = result
     for copy in sent:
         copy.wait_send()
+    for item in w_sent:
+        w_left(*item)
     for name, device in pieces.items():
         remote(name, b_at(0, 0), b_at(0, 0), device).wait_send()
     for name, k, i, device in chunks_sent.values():
@@ -632,6 +708,7 @@
         pltpu.VMEM((4, WCOLS, 2 * block), BF16),
         pltpu.VMEM((width, 2 * block), BF16),
         pltpu.VMEM((width, 2 * block), BF16),
+        pltpu.VMEM((16 * WROWS, 2 * block), F32),
         pltpu.VMEM((16 * WROWS, 2 * block), BF16),
         pltpu.VMEM((16 * WROWS, 2 * block), BF16),
         pltpu.VMEM((2, 16, block), F32),

time: 120 us -> 116 us (0.967)
  Pallas kernels: 118 us -> 114 us
    pallas_call x1, Pallas kernels: 118 us -> 114 us  [per_device(): pl.pallas_call(main_kernel, out_shape=jax.ShapeDtypeStruct((2, NB_SIGMA),...]
where the time goes in v5:
time: 116 us
  Pallas kernels  114 us (98%)
  local copies, waits for them, and re-layouts  1.28 us (1%)
    pallas_call x1, Pallas kernels, per_device(): pl.pallas_call(main_kernel, out_shape=jax.ShapeDtypeStruct((2, NB_SIGMA),...  114 us

profile of v5, /device:TPU:1, one launch (start us, length us, event | category | flops | bytes accessed | tf_op | source)
XLA Modules:
  0.0 115.8 jit_solution(16133548470467980193)
XLA Ops:
  0.0 114.5 %cohsex.1 = f32[2,512]{1,0:T(2,128)} custom-call(s32[5]{0:T(128)} %start_ref.1, s32[5]{0:T(128)} %len_ref.1, s32[5]{0:T(128)} %slot_ref.1, f32[1,128]{1,0:T(1,128)} %bitcast.1, bf16[5,128,2304]{2,1,0:T(8,128)(2,1)} %a_ref.1, bf16[46,2304]{1,0:T(8,128)(2,1)} %eig_ref.1, bf16[736,2944]{1,0:T(8,128)(2,1)} %w_ref.1), custom_call_target="tpu_custom_call" | custom-call | tf_op jit(solution)/shard_map/cohsex/pallas_call | solution.py:727
  114.5 1.3 %copy.9 = f32[2,512]{1,0:T(2,128)} copy(f32[2,512]{1,0:T(2,128)} %cohsex.1) | data formatting | bytes 8192

commit v6 on v5

--- a/solution.py
+++ b/solution.py
@@ -22,7 +22,7 @@
 
 
 WROWS, WCOLS = 96, 768
-N_COPIES = 280
+N_COPIES = 166
 scope = jax.named_scope
 
 
@@ -111,7 +111,7 @@
     for peer in peers:
         pl.semaphore_signal(barrier, inc=1, device_id=peer, device_id_type=pl.DeviceIdType.MESH)
 
-    own_b = pltpu.make_async_copy(eig_ref, share, lsem.at[23])
+    own_b = pltpu.make_async_copy(eig_ref, share, lsem.at[20])
     own_b.start()
     lane = lax.broadcasted_iota(jnp.int32, (1, BLOCK), 1)
     for j in range(5):
@@ -159,6 +159,7 @@
 
     def local(name, src, dst):
         i = local_ids.setdefault(name, len(local_ids))
+        assert i < 20
         copy = pltpu.make_async_copy(src, dst, lsem.at[i])
         copy.start()
         return copy
@@ -644,8 +645,28 @@
                 )
                 spread += jnp.dot(to_rows, wide.astype(BF16), preferred_element_type=F32)
         plane_s[...] = spread.astype(BF16).reshape(4, 4, 16, NB_SIGMA)
+    early = len(sent)
     for (dx, dy), (place, device) in plane.items():
         send(f"plane{dx}{dy}", plane_s.at[place[0], place[1]], plane_r.at[x, y], device)
+    for copy in sent[:early]:
+        copy.wait_send()
+    del sent[:early]
+    for item in w_sent:
+        w_left(*item)
+    for name, device in pieces.items():
+        remote(name, b_at(0, 0), b_at(0, 0), device).wait_send()
+    for name, k, i, device in chunks_sent.values():
+        piece = hop_s.at[i, span(k)]
+        remote(name, piece, piece, device).wait_send()
+    for core in range(2):
+
+        @pl.when(c == core)
+        def _():
+            for name, device in sent_by_core[core]:
+                whole = core == 0 or name in ("by_p", "by_m")
+                piece = b_at(0, 0) if whole else b_half(0, 0, 0)
+                remote(name, piece, piece, device).wait_send()
+
     total = plane_s[x, y].astype(F32)
     for dx, dy in plane:
         source = (x + 4 - dx) % 4, (y + 4 - dy) % 4
@@ -667,23 +688,7 @@
     out_ref[...] = result
     for copy in sent:
         copy.wait_send()
-    for item in w_sent:
-        w_left(*item)
-    for name, device in pieces.items():
-        remote(name, b_at(0, 0), b_at(0, 0), device).wait_send()
-    for name, k, i, device in chunks_sent.values():
-        piece = hop_s.at[i, span(k)]
-        remote(name, piece, piece, device).wait_send()
-    for core in range(2):
-
-        @pl.when(c == core)
-        def _():
-            for name, device in sent_by_core[core]:
-                whole = core == 0 or name in ("by_p", "by_m")
-                piece = b_at(0, 0) if whole else b_half(0, 0, 0)
-                remote(name, piece, piece, device).wait_send()
-
-    assert len(ids) <= N_COPIES
+    assert len(ids) == N_COPIES
 
 
 def per_device(pair_density, eigvecs, screening, occupation, window_start, window_len, slot_band):
@@ -721,7 +726,7 @@
         pltpu.VMEM((2, 4, 2, NB_SIGMA), F32),
         pltpu.SemaphoreType.DMA((N_COPIES,)),
         pltpu.SemaphoreType.DMA((N_COPIES,)),
-        pltpu.SemaphoreType.DMA((24,)),
+        pltpu.SemaphoreType.DMA((21,)),
     ]
     smem = pl.BlockSpec(memory_space=pltpu.SMEM)
     return pl.pallas_call(

time: 116 us -> 114 us (0.983)
  Pallas kernels: 114 us -> 112 us
    pallas_call x1, Pallas kernels: 114 us -> 112 us  [per_device(): pl.pallas_call(main_kernel, out_shape=jax.ShapeDtypeStruct((2, NB_SIGMA),...]
where the time goes in v6:
time: 114 us
  Pallas kernels  112 us (98%)
  local copies, waits for them, and re-layouts  1.28 us (1%)
    pallas_call x1, Pallas kernels, per_device(): pl.pallas_call(main_kernel, out_shape=jax.ShapeDtypeStruct((2, NB_SIGMA),...  112 us

profile of v6, /device:TPU:1, one launch (start us, length us, event | category | flops | bytes accessed | tf_op | source)
XLA Modules:
  0.0 113.5 jit_solution(12164796425059788339)
XLA Ops:
  0.0 112.2 %cohsex.1 = f32[2,512]{1,0:T(2,128)} custom-call(s32[5]{0:T(128)} %start_ref.1, s32[5]{0:T(128)} %len_ref.1, s32[5]{0:T(128)} %slot_ref.1, f32[1,128]{1,0:T(1,128)} %bitcast.1, bf16[5,128,2304]{2,1,0:T(8,128)(2,1)} %a_ref.1, bf16[46,2304]{1,0:T(8,128)(2,1)} %eig_ref.1, bf16[736,2944]{1,0:T(8,128)(2,1)} %w_ref.1), custom_call_target="tpu_custom_call" | custom-call | tf_op jit(solution)/shard_map/cohsex/pallas_call | solution.py:732
  112.2 1.3 %copy.9 = f32[2,512]{1,0:T(2,128)} copy(f32[2,512]{1,0:T(2,128)} %cohsex.1) | data formatting | bytes 8192

commit v7 on v6

--- a/solution.py
+++ b/solution.py
@@ -111,7 +111,7 @@
     for peer in peers:
         pl.semaphore_signal(barrier, inc=1, device_id=peer, device_id_type=pl.DeviceIdType.MESH)
 
-    own_b = pltpu.make_async_copy(eig_ref, share, lsem.at[20])
+    own_b = pltpu.make_async_copy(eig_ref, share, lsem.at[5])
     own_b.start()
     lane = lax.broadcasted_iota(jnp.int32, (1, BLOCK), 1)
     for j in range(5):
@@ -159,7 +159,7 @@
 
     def local(name, src, dst):
         i = local_ids.setdefault(name, len(local_ids))
-        assert i < 20
+        assert i < 4
         copy = pltpu.make_async_copy(src, dst, lsem.at[i])
         copy.start()
         return copy
@@ -484,10 +484,11 @@
     w_got("wzf_p", w_one(2), dev_hm, u, v, "upper")
     w_move("wu_p", w_at(u, v), w_at(u, v), dev_up, u, v)
     w_move("wu_m", w_at(u, v), w_at(u, v), dev_um, u, v)
-    own_w = []
     for p in range(4):
         for q in range(4):
-            own_w.append(local(f"w{p}{q}", w_own(p, q)((0, WROWS), (0, WCOLS)), wbuf.at[0, p, q]))
+            pltpu.make_async_copy(
+                w_own(p, q)((0, WROWS), (0, WCOLS)), wbuf.at[0, p, q], lsem.at[4]
+            ).start()
     combine(2, False, 1)
 
     @pl.when(c == 1)
@@ -570,8 +571,7 @@
         pth[3, :128] = jnp.zeros((128, 2 * BLOCK), BF16)
         pth[3, 128:] = high[3 * WCOLS :, :]
 
-    for copy in own_w:
-        copy.wait()
+    pltpu.make_async_copy(wbuf.at[0], wbuf.at[0], lsem.at[4]).wait()
 
     def screened(rel, q):
         return jnp.dot(
@@ -726,7 +726,7 @@
         pltpu.VMEM((2, 4, 2, NB_SIGMA), F32),
         pltpu.SemaphoreType.DMA((N_COPIES,)),
         pltpu.SemaphoreType.DMA((N_COPIES,)),
-        pltpu.SemaphoreType.DMA((21,)),
+        pltpu.SemaphoreType.DMA((6,)),
     ]
     smem = pl.BlockSpec(memory_space=pltpu.SMEM)
     return pl.pallas_call(

time: 114 us -> 114 us (level)
  no operation moved by 1% of the time
where the time goes in v7:
time: 114 us; the launch traced here: 113 us
  Pallas kernels  112 us (98%)
  local copies, waits for them, and re-layouts  1.28 us (1%)
    pallas_call x1, Pallas kernels, per_device(): pl.pallas_call(main_kernel, out_shape=jax.ShapeDtypeStruct((2, NB_SIGMA),...  112 us

profile of v7, /device:TPU:1, one launch (start us, length us, event | category | flops | bytes accessed | tf_op | source)
XLA Modules:
  0.0 113.4 jit_solution(16465147737493158953)
XLA Ops:
  0.0 112.1 %cohsex.1 = f32[2,512]{1,0:T(2,128)} custom-call(s32[5]{0:T(128)} %start_ref.1, s32[5]{0:T(128)} %len_ref.1, s32[5]{0:T(128)} %slot_ref.1, f32[1,128]{1,0:T(1,128)} %bitcast.1, bf16[5,128,2304]{2,1,0:T(8,128)(2,1)} %a_ref.1, bf16[46,2304]{1,0:T(8,128)(2,1)} %eig_ref.1, bf16[736,2944]{1,0:T(8,128)(2,1)} %w_ref.1), custom_call_target="tpu_custom_call" | custom-call | tf_op jit(solution)/shard_map/cohsex/pallas_call | solution.py:732
  112.1 1.3 %copy.9 = f32[2,512]{1,0:T(2,128)} copy(f32[2,512]{1,0:T(2,128)} %cohsex.1) | data formatting | bytes 8192
